TPU v7x, 128 devices: a whole 4x4x4 slice. The times are simulated.
128 devices in a mesh: grp: 4 (over z), cell: 32 (over x, y, core).
Axes of the slice: x: 4, y: 4, z: 4, core: 2. Of those that a mesh axis runs over, the one named last changes fastest.
Arguments:
- load: float32 [128, 2048, 256], P(('grp', 'cell')), may hold values from -6 to 6
- schur: bfloat16 [128, 2048, 2048], P(('grp', 'cell')), as said below
- local_inverse: bfloat16 [128, 2048, 2048], P(('grp', 'cell')), as said below
- face_map: int32 [128, 4, 512], P(('grp', 'cell')), may hold values from 0 to 511, as said below
- primal_basis: bfloat16 [128, 32, 2048], P(('grp', 'cell')), may hold values from -0.25 to 0.25
- primal_index: int32 [128, 32], P(('grp', 'cell')), may hold values from 0 to 1023
- group_inverse: float32 [4, 1024, 1024], P('grp', 'cell'), as said below
- group_to_coarsest: float32 [4, 1024, 128], P('grp', 'cell'), may hold values from -0.1875 to 0.1875
- coarsest_inverse: float32 [128, 128], replicated, as said below
Outputs:
- solution: float32 [128, 2048, 256], P(('grp', 'cell'))
- residual: float32 [128, 2048, 256], P(('grp', 'cell'))
Inputs may be any that keep to these rules, and one draw needn't show every extreme that they name: face_map[i, f] is a permutation of 0 .. 511, and the maps of two neighbouring cells across their shared face are inverse to each other. `schur`: each cell's matrix is symmetric positive definite. `local_inverse`: each cell's matrix is symmetric positive definite. `group_inverse`: each row's matrix is symmetric positive definite. `coarsest_inverse`: symmetric positive definite.
All inputs are finite; a program needn't handle non-finite values.
Results may differ from a plain program's by a relative error of at most 0.0066.
Values sent between devices are 32-bit elements; how exact they have to be, the bound alone decides.
A program may use at most 128 MiB of HBM per device.

v0:
```python
import jax
import jax.numpy as jnp
from jax import lax
from jax.sharding import Mesh
from jax.sharding import PartitionSpec as P

ITERS = 2
CELL = ("cell_0", "cell_1", "cell_2")
GRP_CELL = ("grp", "cell_0", "cell_1", "cell_2")


HIGHEST = lax.Precision.HIGHEST


def extended(cells, sides, width):
    for axis, dim in sides:
        count = lax.axis_size(axis)
        ends = count - 1
        head = lax.slice_in_dim(cells, 0, width, axis=dim)
        tail = lax.slice_in_dim(cells, cells.shape[dim] - width, cells.shape[dim], axis=dim)
        cells = jnp.concatenate(
            [
                lax.ppermute(tail, axis, [(i, (i + 1) % count) for i in range(ends)]),
                cells,
                lax.ppermute(head, axis, [((i + 1) % count, i) for i in range(ends)]),
            ],
            axis=dim,
        )
    return cells


def copy_for_each(array, axis):
    copies = jnp.broadcast_to(array, (lax.axis_size(axis), *array.shape))
    return lax.all_to_all(copies, axis, split_axis=0, concat_axis=0, tiled=True)


def over_copies(array, axis):
    return copy_for_each(array, axis).sum(axis=0)


def by_axis(array, axes):
    far, near = axes
    nearer = over_copies(array, near)
    return over_copies(nearer, far)


def split_up(array, dim, count):
    lengths = array.shape
    blocks = array.reshape(*lengths[:dim], count, lengths[dim] // count, *lengths[dim + 1 :])
    return jnp.moveaxis(blocks, dim, 0)


def summed_on_arrival(array, axis, dim):
    count = lax.axis_size(axis)
    blocks = lax.all_to_all(split_up(array, dim, count), axis, 0, 0, tiled=True)
    return jnp.sum(blocks, axis=0)


def filled_up(lines, count):
    spare = -lines.shape[0] % count
    if not spare:
        return lines
    return jnp.concatenate([lines, jnp.zeros((spare, *lines.shape[1:]), lines.dtype)])


def joined_along(blocks, dim):
    blocks = jnp.moveaxis(blocks, 0, dim)
    lengths = blocks.shape
    return blocks.reshape(*lengths[:dim], lengths[dim] * lengths[dim + 1], *lengths[dim + 2 :])


def whole_of(array, axes, dim):
    far, near = axes
    leading = copy_for_each(array, far)
    blocks = jnp.swapaxes(copy_for_each(leading, near), 0, 1)
    return joined_along(blocks.reshape(-1, *array.shape), dim)


def sum_in_two_steps(array, axes, dim):
    far, near = axes
    own = summed_on_arrival(split_up(array, dim, lax.axis_size(far)), near, dim + 1)
    return jnp.sum(lax.all_to_all(own, far, 0, 0, tiled=True), axis=0)


def nested_sum(array, axes):
    lines = array.reshape(-1, array.shape[-1])
    padded = filled_up(lines, lax.axis_size(axes[0]) * lax.axis_size(axes[1]))
    whole = whole_of(sum_in_two_steps(padded, axes, 0), axes, 0)
    return lax.slice_in_dim(whole, 0, len(lines)).reshape(array.shape)


def gathered_copies(array, axis, dim):
    return joined_along(copy_for_each(array, axis), dim)


def face_weights(ifaces):
    grp_index = lax.axis_index("grp")
    cell_index = lax.axis_index(CELL)
    exists = jnp.stack(
        [
            cell_index > 0,
            cell_index < lax.axis_size(CELL) - 1,
            grp_index > 0,
            grp_index < lax.axis_size("grp") - 1,
        ]
    )
    per_face = jnp.where(exists, 0.5, 1.0).astype(jnp.float32)
    return jnp.repeat(per_face, ifaces // 4)[:, None]


def assemble(values, mapping):
    faces = values.reshape(4, values.shape[0] // 4, values.shape[1])
    across_cell = extended(faces[0:2], ((CELL, 0),), 1)
    across_grp = extended(faces[2:4], (("grp", 0),), 1)
    received = jnp.stack([across_cell[0], across_cell[3], across_grp[0], across_grp[3]])
    moved = jax.vmap(lambda block, order: block[order])(received, mapping)
    return values + moved.reshape(values.shape)


def inner(term):
    return by_axis(jnp.sum(term, axis=0), (("grp", "cell_0", "cell_1"), "cell_2"))


def precondition(
    residual, weight_rows, local_matrix, basis, onehot, row_inverse, lifting, coarsest_inverse
):
    weighted = (residual * weight_rows).astype(jnp.bfloat16)
    local_part = jnp.dot(local_matrix, weighted, preferred_element_type=jnp.float32)
    primal = jnp.dot(basis, weighted, preferred_element_type=jnp.float32)
    coarse_local = jnp.dot(onehot.T, primal, precision=HIGHEST)
    owned = summed_on_arrival(coarse_local, CELL, 0)
    coarsest = nested_sum(
        jnp.dot(lifting.T, owned, precision=HIGHEST), (("grp", "cell_0", "cell_1"), "cell_2")
    )
    coarsest_solution = jnp.dot(coarsest_inverse, coarsest, precision=HIGHEST)
    lifted = jnp.dot(lifting, coarsest_solution, precision=HIGHEST)
    owned_solution = lifted + jnp.dot(
        row_inverse, gathered_copies(owned, CELL, 0), precision=HIGHEST
    )
    row_solution = gathered_copies(owned_solution, CELL, 0)
    picked = jnp.dot(onehot, row_solution, precision=HIGHEST)
    coarse_part = jnp.dot(basis.astype(jnp.float32).T, picked, precision=HIGHEST)
    return (local_part + coarse_part) * weight_rows


def body(
    load,
    schur,
    local_inverse,
    face_map,
    primal_basis,
    primal_index,
    group_inverse,
    group_to_coarsest,
    coarsest_inverse,
):
    ifaces = load.shape[1]
    row_unknowns = group_inverse.shape[2]
    weight_rows = face_weights(ifaces)
    mapping = face_map[0]
    onehot = (primal_index[0][:, None] == lax.iota(jnp.int32, row_unknowns)[None, :]).astype(
        jnp.float32
    )
    matrix = schur[0]

    def apply_pre(values):
        scaled = precondition(
            values,
            weight_rows,
            local_inverse[0],
            primal_basis[0],
            onehot,
            group_inverse[0],
            group_to_coarsest[0],
            coarsest_inverse,
        )
        return assemble(scaled, mapping)

    rhs_side = assemble(load[0], mapping)
    solution = jnp.zeros_like(rhs_side)
    residual = rhs_side
    search = apply_pre(residual)
    direction = search
    product = inner(weight_rows * residual * search)
    for iteration in range(ITERS):
        image_local = jnp.dot(
            matrix, direction.astype(jnp.bfloat16), preferred_element_type=jnp.float32
        )
        curvature = inner(direction * image_local)
        image = assemble(image_local, mapping)
        alpha = product / curvature
        solution = solution + alpha * direction
        residual = residual - alpha * image
        if iteration + 1 < ITERS:
            search = apply_pre(residual)
            product_next = inner(weight_rows * residual * search)
            direction = search + product_next / product * direction
            product = product_next
    return (solution[None], residual[None])


def solution(mesh):
    torus = Mesh(
        mesh.devices.reshape(mesh.shape["grp"], 4, 4, 2), ("grp", "cell_0", "cell_1", "cell_2")
    )
    in_specs = (
        P(GRP_CELL, None, None),
        P(GRP_CELL, None, None),
        P(GRP_CELL, None, None),
        P(GRP_CELL, None, None),
        P(GRP_CELL, None, None),
        P(GRP_CELL, None),
        P("grp", CELL, None),
        P("grp", CELL, None),
        P(),
    )
    out_specs = (P(GRP_CELL, None, None), P(GRP_CELL, None, None))
    return jax.shard_map(body, mesh=torus, in_specs=in_specs, out_specs=out_specs, check_vma=False)
```

profile of v0, /device:TPU:1, one launch (start us, length us, event | category | flops | bytes accessed | tf_op | source)
XLA Modules:
  0.0 592.2 jit_solution(1990529903516253283)
XLA Ops:
  3.2 4.6 collective-permute-start
  7.8 3.6 collective-permute-start.2
  14.8 7.4 %collective-permute-done.2 = f32[1,512,256]{2,1,0:T(8,128)S(1)} collective-permute-done((f32[1,512,256]{2,1,0:T(8,128)S(1)}, f32[1,512,256]{2,1,0:T(8,128)S(1)}, u32[]{:S(2)}, u32[]{:S(2)}) %collective-permute-start.2) | collective-permute-done | bytes 524320 | tf_op jit(solution)/shard_map/ppermute | solution.py:23
  23.1 4.7 collective-permute-done.3
  29.2 23.9 %gather_fusion = f32[2048,256]{1,0:T(8,128)} fusion(f32[4,512,256]{2,1,0:T(8,128)S(1)} %pad_maximum_fusion, s32[2048]{0:T(1024)S(1)} %bitcast.165), kind=kCustom, calls=%fused_computation | custom fusion | bytes 4210688 | tf_op jit(solution)/shard_map/vmap()/gather | solution.py:116
  56.7 25.6 %all_to_all.124 = f32[32,32,256]{2,1,0:T(8,128)S(1)} all-to-all(f32[32,32,256]{2,1,0:T(8,128)S(1)} %bitcast.174), channel_id=1, replica_groups=mesh['grp'=4,'cell_0'=4,'cell_1'=4,'cell_2'=2] {'cell_0','cell_1','cell_2'}, dimensions={0} | all-to-all | bytes 2097152 | tf_op jit(solution)/shard_map/all_to_all | solution.py:55
  82.7 3.6 all_to_all.125
  86.4 15.6 %all_to_all.126 = f32[64,1,256]{2,1,0:T(1,128)S(1)} all-to-all(f32[64,1,256]{2,1,0:T(1,128)S(1)} %reduce_sum.168), channel_id=1, replica_groups=mesh['grp'=4,'cell_0'=4,'cell_1'=4,'cell_2'=2] {'grp','cell_0','cell_1'}, dimensions={0} | all-to-all | bytes 131072 | tf_op jit(solution)/shard_map/all_to_all | solution.py:82
  102.1 13.3 %all_to_all.127 = f32[64,1,256]{2,1,0:T(1,128)S(1)} all-to-all(f32[64,1,256]{2,1,0:T(1,128)S(1)} %broadcast_in_dim.79), channel_id=1, replica_groups=mesh['grp'=4,'cell_0'=4,'cell_1'=4,'cell_2'=2] {'grp','cell_0','cell_1'}, dimensions={0} | all-to-all | bytes 131072 | tf_op jit(solution)/shard_map/all_to_all | solution.py:34
  115.5 6.4 %all_to_all.128 = f32[2,64,1,256]{3,1,2,0:T(8,128)S(1)} all-to-all(f32[2,64,1,256]{3,1,2,0:T(8,128)S(1)} %broadcast_in_dim.80), channel_id=1, replica_groups=mesh['grp'=4,'cell_0'=4,'cell_1'=4,'cell_2'=2] {'cell_2'}, dimensions={0} | all-to-all | bytes 262144 | tf_op jit(solution)/shard_map/all_to_all | solution.py:34
  123.0 3.9 all-to-all-start.5
  127.8 16.1 %all-to-all-done.5 = f32[32,32,256]{2,1,0:T(8,128)S(1)} async-done(((f32[32,32,256]{2,1,0:T(8,128)}), f32[32,32,256]{2,1,0:T(8,128)S(1)}, u32[]{:S(2)}, u32[]{:S(2)}) %all-to-all-start.5) | async-done | bytes 1048608 | tf_op jit(solution)/shard_map/all_to_all | solution.py:34
  145.7 4.2 all-to-all-start.6
  149.9 7.2 %fusion.6 = f32[256,2048]{1,0:T(8,128)} fusion(bf16[2048,256]{1,0:T(8,128)(2,1)S(1)} %fusion.22, bf16[1,2048,2048]{2,1,0:T(8,128)(2,1)} %param.11), kind=kOutput, calls=%fused_computation.11 | convolution fusion | flops 2147483648 | bytes 11534336 | tf_op jit(solution)/shard_map/dot_general | solution.py:128
  157.1 9.6 %all-to-all-done.6 = f32[32,32,256]{2,1,0:T(8,128)S(1)} async-done(((f32[32,32,256]{2,1,0:T(8,128)}), f32[32,32,256]{2,1,0:T(8,128)S(1)}, u32[]{:S(2)}, u32[]{:S(2)}) %all-to-all-start.6) | async-done | bytes 1048608 | tf_op jit(solution)/shard_map/all_to_all | solution.py:34
  167.2 2.7 fusion.17
  175.3 4.8 collective-permute-start.6
  180.1 2.8 collective-permute-start.5
  182.9 2.9 copy.67
  190.8 3.0 pad_maximum_fusion.1
  195.7 23.9 %gather_fusion.1 = f32[2048,256]{1,0:T(8,128)} fusion(f32[4,512,256]{2,1,0:T(8,128)S(1)} %copy.71, s32[2048]{0:T(1024)S(1)} %bitcast.166), kind=kCustom, calls=%fused_computation.1 | custom fusion | bytes 4210688 | tf_op jit(solution)/shard_map/vmap()/gather | solution.py:116
  219.6 3.1 copy.72
  225.5 6.7 %multiply_reduce_fusion.2 = (f32[256]{0:T(256)S(1)}, f32[256]{0:T(256)S(1)}, f32[2048,256]{0,1:T(8,128)S(1)}) fusion(f32[2048,256]{0,1:T(8,128)S(1)} %add.73, f32[2048,256]{0,1:T(8,128)S(1)} %copy-done.10, f32[1,2048,256]{1,2,0:T(8,128)S(1)} %copy-done.9, f32[2048]{0:T(1024)S(1)} %bitcast.182, bf16[1,2048,2048]{2,1,0:T(8,128)(2,1)} %param.10), kind=kOutput, calls=%fused_computation.36 | convolution fusion | flops 2151153152 | bytes 16787456 | tf_op jit(solution)/shard_map/dot_general | solution.py:186
  233.7 3.5 collective-permute-start.8
  238.6 4.8 collective-permute-start.10
  245.3 3.4 all_to_all.129
  249.2 3.5 all-to-all-start.7
  254.4 8.2 %all-to-all-start.10 = ((f32[64,1,256]{2,1,0:T(1,128)}), f32[64,1,256]{2,1,0:T(1,128)S(1)}, u32[]{:S(2)}, u32[]{:S(2)}) async-start(f32[64,1,256]{2,1,0:T(1,128)} %broadcast_in_dim.86), calls=%async_computation.10 | async-start | bytes 131072 | tf_op jit(solution)/shard_map/all_to_all | solution.py:34
  262.6 8.4 %all-to-all-done.10 = f32[64,1,256]{2,1,0:T(1,128)S(1)} async-done(((f32[64,1,256]{2,1,0:T(1,128)}), f32[64,1,256]{2,1,0:T(1,128)S(1)}, u32[]{:S(2)}, u32[]{:S(2)}) %all-to-all-start.10) | async-done | bytes 65568 | tf_op jit(solution)/shard_map/all_to_all | solution.py:34
  271.7 5.2 all-to-all-start.8
  277.6 7.9 %all-to-all-done.8 = f32[64,1,256]{2,1,0:T(1,128)S(1)} async-done(((f32[64,1,256]{2,1,0:T(1,128)}), f32[64,1,256]{2,1,0:T(1,128)S(1)}, u32[]{:S(2)}, u32[]{:S(2)}) %all-to-all-start.8) | async-done | bytes 65568 | tf_op jit(solution)/shard_map/all_to_all | solution.py:34
  286.2 2.6 pad_maximum_fusion.2
  290.8 23.9 %gather_fusion.2 = f32[2048,256]{1,0:T(8,128)} fusion(f32[4,512,256]{2,1,0:T(8,128)S(1)} %copy.77, s32[2048]{0:T(1024)S(1)} %bitcast.167), kind=kCustom, calls=%fused_computation.2 | custom fusion | bytes 4210688 | tf_op jit(solution)/shard_map/vmap()/gather | solution.py:116
  314.7 2.9 copy.78
  317.6 4.4 multiply_subtract_fusion
  323.4 23.0 %all_to_all.130 = f32[32,32,256]{2,1,0:T(8,128)S(1)} all-to-all(f32[32,32,256]{2,1,0:T(8,128)S(1)} %bitcast.175), channel_id=1, replica_groups=mesh['grp'=4,'cell_0'=4,'cell_1'=4,'cell_2'=2] {'cell_0','cell_1','cell_2'}, dimensions={0} | all-to-all | bytes 2097152 | tf_op jit(solution)/shard_map/all_to_all | solution.py:55
  346.9 3.6 all_to_all.131
  350.5 13.5 %all_to_all.132 = f32[64,1,256]{2,1,0:T(1,128)S(1)} all-to-all(f32[64,1,256]{2,1,0:T(1,128)S(1)} %reduce_sum.178), channel_id=1, replica_groups=mesh['grp'=4,'cell_0'=4,'cell_1'=4,'cell_2'=2] {'grp','cell_0','cell_1'}, dimensions={0} | all-to-all | bytes 131072 | tf_op jit(solution)/shard_map/all_to_all | solution.py:82
  364.2 13.3 %all_to_all.133 = f32[64,1,256]{2,1,0:T(1,128)S(1)} all-to-all(f32[64,1,256]{2,1,0:T(1,128)S(1)} %broadcast_in_dim.87), channel_id=1, replica_groups=mesh['grp'=4,'cell_0'=4,'cell_1'=4,'cell_2'=2] {'grp','cell_0','cell_1'}, dimensions={0} | all-to-all | bytes 131072 | tf_op jit(solution)/shard_map/all_to_all | solution.py:34
  377.5 6.4 %all_to_all.134 = f32[2,64,1,256]{3,1,2,0:T(8,128)S(1)} all-to-all(f32[2,64,1,256]{3,1,2,0:T(8,128)S(1)} %broadcast_in_dim.88), channel_id=1, replica_groups=mesh['grp'=4,'cell_0'=4,'cell_1'=4,'cell_2'=2] {'cell_2'}, dimensions={0} | all-to-all | bytes 262144 | tf_op jit(solution)/shard_map/all_to_all | solution.py:34
  385.8 3.9 all-to-all-start.16
  393.7 13.1 %all-to-all-done.16 = f32[32,32,256]{2,1,0:T(8,128)S(1)} async-done(((f32[32,32,256]{2,1,0:T(8,128)}), f32[32,32,256]{2,1,0:T(8,128)S(1)}, u32[]{:S(2)}, u32[]{:S(2)}) %all-to-all-start.16) | async-done | bytes 1048608 | tf_op jit(solution)/shard_map/all_to_all | solution.py:34
  408.5 4.3 all-to-all-start.17
  412.8 7.1 %fusion.4 = f32[256,2048]{1,0:T(8,128)} fusion(bf16[1,2048,2048]{2,1,0:T(8,128)(2,1)} %param.11, f32[2048,256]{0,1:T(8,128)S(1)} %multiply_subtract_fusion, f32[2048]{0:T(1024)S(1)} %bitcast.184), kind=kOutput, calls=%fused_computation.9 | convolution fusion | flops 2148532224 | bytes 12591104 | tf_op jit(solution)/shard_map/dot_general | solution.py:128
  419.9 9.7 %all-to-all-done.17 = f32[32,32,256]{2,1,0:T(8,128)S(1)} async-done(((f32[32,32,256]{2,1,0:T(8,128)}), f32[32,32,256]{2,1,0:T(8,128)S(1)}, u32[]{:S(2)}, u32[]{:S(2)}) %all-to-all-start.17) | async-done | bytes 1048608 | tf_op jit(solution)/shard_map/all_to_all | solution.py:34
  430.1 2.7 fusion.15
  437.6 4.0 collective-permute-start.14
  441.6 2.7 collective-permute-start.13
  444.4 7.0 %collective-permute-done.15 = f32[1,512,256]{1,2,0:T(8,128)S(1)} collective-permute-done((f32[1,512,256]{1,2,0:T(8,128)S(1)}, f32[1,512,256]{1,2,0:T(8,128)S(1)}, u32[]{:S(2)}, u32[]{:S(2)}) %collective-permute-start.15) | collective-permute-done | bytes 524320 | tf_op jit(solution)/shard_map/ppermute | solution.py:25
  455.8 23.8 %gather_fusion.3 = f32[2048,256]{1,0:T(8,128)} fusion(f32[4,512,256]{2,1,0:T(8,128)S(1)} %copy.81, s32[2048]{0:T(1024)S(1)} %bitcast.168), kind=kCustom, calls=%fused_computation.3 | custom fusion | bytes 4210688 | tf_op jit(solution)/shard_map/vmap()/gather | solution.py:116
  479.5 3.1 copy.82
  482.6 4.1 multiply_reduce_fusion.1
  486.7 4.7 all_to_all.135
  491.5 16.1 %all_to_all.136 = f32[64,1,256]{2,1,0:T(1,128)S(1)} all-to-all(f32[64,1,256]{2,1,0:T(1,128)S(1)} %broadcast_in_dim.92), channel_id=1, replica_groups=mesh['grp'=4,'cell_0'=4,'cell_1'=4,'cell_2'=2] {'grp','cell_0','cell_1'}, dimensions={0} | all-to-all | bytes 131072 | tf_op jit(solution)/shard_map/all_to_all | solution.py:34
  507.7 8.4 %multiply_reduce_fusion = (f32[256]{0:T(256)S(1)}, f32[2048,256]{0,1:T(8,128)S(1)}) fusion(f32[2048,256]{0,1:T(8,128)} %get-tuple-element.15, f32[2048,256]{0,1:T(8,128)} %copy-done.8, f32[256]{0:T(256)S(1)} %div.22, bf16[1,2048,2048]{2,1,0:T(8,128)(2,1)} %param.10), kind=kOutput, calls=%fused_computation.32 | convolution fusion | flops 2151153408 | bytes 14682112 | tf_op jit(solution)/shard_map/dot_general | solution.py:186
  517.6 3.8 collective-permute-start.16
  522.7 4.0 collective-permute-start.18
  528.7 3.4 all_to_all.137
  532.1 16.5 %all_to_all.138 = f32[64,1,256]{2,1,0:T(1,128)S(1)} all-to-all(f32[64,1,256]{2,1,0:T(1,128)S(1)} %broadcast_in_dim.94), channel_id=1, replica_groups=mesh['grp'=4,'cell_0'=4,'cell_1'=4,'cell_2'=2] {'grp','cell_0','cell_1'}, dimensions={0} | all-to-all | bytes 131072 | tf_op jit(solution)/shard_map/all_to_all | solution.py:34
  548.7 2.6 pad_maximum_fusion.4
  553.3 23.8 %gather_fusion.4 = f32[2048,256]{1,0:T(8,128)} fusion(f32[4,512,256]{2,1,0:T(8,128)S(1)} %copy.87, s32[2048]{0:T(1024)S(1)} %bitcast.169), kind=kCustom, calls=%fused_computation.4 | custom fusion | bytes 4210688 | tf_op jit(solution)/shard_map/vmap()/gather | solution.py:116
  577.1 3.1 copy.88
  580.2 6.6 %subtract_bitcast_fusion = (f32[1,2048,256]{1,2,0:T(8,128)}, f32[1,2048,256]{1,2,0:T(8,128)}) fusion(f32[2048,256]{0,1:T(8,128)S(1)} %copy-done.3, f32[2048,256]{0,1:T(8,128)} %copy-done.12, f32[2048,256]{0,1:T(8,128)} %copy.88, f32[256]{0:T(256)S(1)} %div.23, f32[2048,256]{0,1:T(8,128)} %get-tuple-element.15, f32[2048,256]{0,1:T(8,128)} %copy-done.8, ...), kind=kLoop, calls=%fused_computation.30 | loop fusion | flops 4194304 | bytes 14683136 | tf_op jit(solution)/shard_map/broadcast_in_dim | solution.py:199
  586.8 3.0 copy.90
  (163 shorter events, 70.7 us)
Async XLA Ops:
  0.6 55.0 %copy-start = (bf16[1,32,2048]{2,1,0:T(8,128)(2,1)S(1)}, bf16[1,32,2048]{2,1,0:T(8,128)(2,1)}, u32[]{:S(2)}) copy-start(bf16[1,32,2048]{2,1,0:T(8,128)(2,1)} %param.13) | copy-start | bytes 393220
  0.6 14.1 %copy-start.27 = (s32[1,4,512]{2,1,0:T(4,128)S(1)}, s32[1,4,512]{2,1,0:T(4,128)}, u32[]{:S(2)}) copy-start(s32[1,4,512]{2,1,0:T(4,128)} %param.12) | copy-start | bytes 24580
  3.2 11.6 %collective-permute-start = (f32[1,512,256]{2,1,0:T(8,128)}, f32[1,512,256]{2,1,0:T(8,128)S(1)}, u32[]{:S(2)}, u32[]{:S(2)}) collective-permute-start(f32[1,512,256]{2,1,0:T(8,128)} %get-tuple-element.32), channel_id=1, source_target_pairs={{0,1},{1,2},{2,3},{3,4},{4,5},{5,6},{6,7},{7,8},{8,9},{9,10},{10,1... | collective-permute-start | bytes 1572872 | tf_op jit(solution)/shard_map/ppermute | solution.py:23
  7.8 14.4 %collective-permute-start.2 = (f32[1,512,256]{2,1,0:T(8,128)S(1)}, f32[1,512,256]{2,1,0:T(8,128)S(1)}, u32[]{:S(2)}, u32[]{:S(2)}) collective-permute-start(f32[1,512,256]{2,1,0:T(8,128)S(1)} %get-tuple-element.33), channel_id=1, source_target_pairs={{0,32},{32,64},{64,96},{1,33},{33,65},{65,97},{2,34},{34,66},{66,9... | collective-permute-start | bytes 1572872 | tf_op jit(solution)/shard_map/ppermute | solution.py:23
  11.4 10.9 %collective-permute-start.1 = (f32[1,512,256]{2,1,0:T(8,128)S(1)}, f32[1,512,256]{2,1,0:T(8,128)S(1)}, u32[]{:S(2)}, u32[]{:S(2)}) collective-permute-start(f32[1,512,256]{2,1,0:T(8,128)S(1)} %get-tuple-element.34), channel_id=1, source_target_pairs={{1,0},{2,1},{3,2},{4,3},{5,4},{6,5},{7,6},{8,7},{9,8},{10,9},{11,1... | collective-permute-start | bytes 1572872 | tf_op jit(solution)/shard_map/ppermute | solution.py:25
  13.3 14.4 %collective-permute-start.3 = (f32[1,512,256]{2,1,0:T(8,128)S(1)}, f32[1,512,256]{2,1,0:T(8,128)}, u32[]{:S(2)}, u32[]{:S(2)}) collective-permute-start(f32[1,512,256]{2,1,0:T(8,128)S(1)} %get-tuple-element.35), channel_id=1, source_target_pairs={{32,0},{64,32},{96,64},{33,1},{65,33},{97,65},{34,2},{66,34},{98,6... | collective-permute-start | bytes 1572872 | tf_op jit(solution)/shard_map/ppermute | solution.py:25
  22.3 0.8 copy-start.15
  53.1 2.9 copy-start.24
  56.0 26.3 %copy-start.18 = (f32[1,32,128]{2,1,0:T(8,128)S(1)}, f32[1,32,128]{2,1,0:T(8,128)}, u32[]{:S(2)}) copy-start(f32[1,32,128]{2,1,0:T(8,128)} %param.16) | copy-start | bytes 49156
  115.5 11.7 %copy-start.17 = (f32[128,128]{1,0:T(8,128)S(1)}, f32[128,128]{1,0:T(8,128)}, u32[]{:S(2)}) copy-start(f32[128,128]{1,0:T(8,128)} %param.17) | copy-start | bytes 196612
  121.9 22.0 %copy-start.14 = (f32[1,32,1024]{2,1,0:T(8,128)S(1)}, f32[1,32,1024]{2,1,0:T(8,128)}, u32[]{:S(2)}) copy-start(f32[1,32,1024]{2,1,0:T(8,128)} %param.15) | copy-start | bytes 393220
  123.0 20.9 %all-to-all-start.5 = ((f32[32,32,256]{2,1,0:T(8,128)}), f32[32,32,256]{2,1,0:T(8,128)S(1)}, u32[]{:S(2)}, u32[]{:S(2)}) async-start(f32[32,32,256]{2,1,0:T(8,128)} %broadcast_in_dim.81), calls=%async_computation.5 | async-start | bytes 2097152 | tf_op jit(solution)/shard_map/all_to_all | solution.py:34
  145.7 21.0 %all-to-all-start.6 = ((f32[32,32,256]{2,1,0:T(8,128)}), f32[32,32,256]{2,1,0:T(8,128)S(1)}, u32[]{:S(2)}, u32[]{:S(2)}) async-start(f32[32,32,256]{2,1,0:T(8,128)} %broadcast_in_dim.82), calls=%async_computation.6 | async-start | bytes 2097152 | tf_op jit(solution)/shard_map/all_to_all | solution.py:34
  170.0 1.8 copy-start.5
  171.8 15.9 %collective-permute-start.4 = (f32[1,512,256]{1,2,0:T(8,128)}, f32[1,512,256]{1,2,0:T(8,128)S(1)}, u32[]{:S(2)}, u32[]{:S(2)}) collective-permute-start(f32[1,512,256]{1,2,0:T(8,128)} %get-tuple-element.28), channel_id=1, source_target_pairs={{0,1},{1,2},{2,3},{3,4},{4,5},{5,6},{6,7},{7,8},{8,9},{9,10},{10,1... | collective-permute-start | bytes 1572872 | tf_op jit(solution)/shard_map/ppermute | solution.py:23
  174.0 15.4 %collective-permute-start.7 = (f32[1,512,256]{1,2,0:T(8,128)}, f32[1,512,256]{1,2,0:T(8,128)}, u32[]{:S(2)}, u32[]{:S(2)}) collective-permute-start(f32[1,512,256]{1,2,0:T(8,128)} %get-tuple-element.29), channel_id=1, source_target_pairs={{32,0},{64,32},{96,64},{33,1},{65,33},{97,65},{34,2},{66,34},{98,6... | collective-permute-start | bytes 1572872 | tf_op jit(solution)/shard_map/ppermute | solution.py:25
  175.3 15.0 %collective-permute-start.6 = (f32[1,512,256]{1,2,0:T(8,128)}, f32[1,512,256]{1,2,0:T(8,128)}, u32[]{:S(2)}, u32[]{:S(2)}) collective-permute-start(f32[1,512,256]{1,2,0:T(8,128)} %get-tuple-element.30), channel_id=1, source_target_pairs={{0,32},{32,64},{64,96},{1,33},{33,65},{65,97},{2,34},{34,66},{66,9... | collective-permute-start | bytes 1572872 | tf_op jit(solution)/shard_map/ppermute | solution.py:23
  180.1 5.8 copy-start.4
  180.1 10.7 %collective-permute-start.5 = (f32[1,512,256]{1,2,0:T(8,128)S(1)}, f32[1,512,256]{1,2,0:T(8,128)}, u32[]{:S(2)}, u32[]{:S(2)}) collective-permute-start(f32[1,512,256]{1,2,0:T(8,128)S(1)} %get-tuple-element.31), channel_id=1, source_target_pairs={{1,0},{2,1},{3,2},{4,3},{5,4},{6,5},{7,6},{8,7},{9,8},{10,9},{11,1... | collective-permute-start | bytes 1572872 | tf_op jit(solution)/shard_map/ppermute | solution.py:25
  219.6 3.1 copy-start.6
  222.6 2.2 copy-start.9
  222.6 2.9 copy-start.10
  225.5 6.7 %copy-start.8 = (f32[2048,256]{0,1:T(8,128)}, f32[2048,256]{0,1:T(8,128)S(1)}, u32[]{:S(2)}) copy-start(f32[2048,256]{0,1:T(8,128)S(1)} %add.73) | copy-start | bytes 6291460
  232.2 1.5 copy-start.11
  233.7 52.5 %collective-permute-start.8 = (f32[1,512,256]{1,2,0:T(8,128)}, f32[1,512,256]{1,2,0:T(8,128)S(1)}, u32[]{:S(2)}, u32[]{:S(2)}) collective-permute-start(f32[1,512,256]{1,2,0:T(8,128)} %get-tuple-element.24), channel_id=1, source_target_pairs={{0,1},{1,2},{2,3},{3,4},{4,5},{5,6},{6,7},{7,8},{8,9},{9,10},{10,1... | collective-permute-start | bytes 1572872 | tf_op jit(solution)/shard_map/ppermute | solution.py:23
  237.3 48.9 %collective-permute-start.11 = (f32[1,512,256]{1,2,0:T(8,128)S(1)}, f32[1,512,256]{1,2,0:T(8,128)S(1)}, u32[]{:S(2)}, u32[]{:S(2)}) collective-permute-start(f32[1,512,256]{1,2,0:T(8,128)S(1)} %get-tuple-element.25), channel_id=1, source_target_pairs={{32,0},{64,32},{96,64},{33,1},{65,33},{97,65},{34,2},{66,34},{98,6... | collective-permute-start | bytes 1572872 | tf_op jit(solution)/shard_map/ppermute | solution.py:25
  238.6 47.7 %collective-permute-start.10 = (f32[1,512,256]{1,2,0:T(8,128)S(1)}, f32[1,512,256]{1,2,0:T(8,128)S(1)}, u32[]{:S(2)}, u32[]{:S(2)}) collective-permute-start(f32[1,512,256]{1,2,0:T(8,128)S(1)} %get-tuple-element.26), channel_id=1, source_target_pairs={{0,32},{32,64},{64,96},{1,33},{33,65},{65,97},{2,34},{34,66},{66,9... | collective-permute-start | bytes 1572872 | tf_op jit(solution)/shard_map/ppermute | solution.py:23
  243.3 42.9 %collective-permute-start.9 = (f32[1,512,256]{1,2,0:T(8,128)S(1)}, f32[1,512,256]{1,2,0:T(8,128)}, u32[]{:S(2)}, u32[]{:S(2)}) collective-permute-start(f32[1,512,256]{1,2,0:T(8,128)S(1)} %get-tuple-element.27), channel_id=1, source_target_pairs={{1,0},{2,1},{3,2},{4,3},{5,4},{6,5},{7,6},{8,7},{9,8},{10,9},{11,1... | collective-permute-start | bytes 1572872 | tf_op jit(solution)/shard_map/ppermute | solution.py:25
  249.2 4.6 all-to-all-start.7
  254.4 16.6 %all-to-all-start.10 = ((f32[64,1,256]{2,1,0:T(1,128)}), f32[64,1,256]{2,1,0:T(1,128)S(1)}, u32[]{:S(2)}, u32[]{:S(2)}) async-start(f32[64,1,256]{2,1,0:T(1,128)} %broadcast_in_dim.86), calls=%async_computation.10 | async-start | bytes 131072 | tf_op jit(solution)/shard_map/all_to_all | solution.py:34
  271.7 13.7 %all-to-all-start.8 = ((f32[64,1,256]{2,1,0:T(1,128)}), f32[64,1,256]{2,1,0:T(1,128)S(1)}, u32[]{:S(2)}, u32[]{:S(2)}) async-start(f32[64,1,256]{2,1,0:T(1,128)} %broadcast_in_dim.84), calls=%async_computation.8 | async-start | bytes 131072 | tf_op jit(solution)/shard_map/all_to_all | solution.py:34
  285.5 3.3 copy-start.20
  286.2 31.4 %copy-start.22 = (f32[256]{0:T(256)}, f32[256]{0:T(256)S(1)}, u32[]{:S(2)}) copy-start(f32[256]{0:T(256)S(1)} %div.21) | copy-start | bytes 3076
  322.0 90.8 %copy-start.1 = (f32[2048,256]{0,1:T(8,128)}, f32[2048,256]{0,1:T(8,128)S(1)}, u32[]{:S(2)}) copy-start(f32[2048,256]{0,1:T(8,128)S(1)} %multiply_subtract_fusion) | copy-start | bytes 6291460
  322.0 0.7 copy-start.25
  322.7 23.8 %copy-start.19 = (f32[1,32,128]{2,1,0:T(8,128)S(1)}, f32[1,32,128]{2,1,0:T(8,128)}, u32[]{:S(2)}) copy-start(f32[1,32,128]{2,1,0:T(8,128)} %param.16) | copy-start | bytes 49156
  346.5 31.1 %copy-start.16 = (f32[32,256]{1,0:T(8,128)}, f32[32,256]{1,0:T(8,128)S(1)}, u32[]{:S(2)}) copy-start(f32[32,256]{1,0:T(8,128)S(1)} %reduce_sum.176) | copy-start | bytes 98308
  385.8 20.9 %all-to-all-start.16 = ((f32[32,32,256]{2,1,0:T(8,128)}), f32[32,32,256]{2,1,0:T(8,128)S(1)}, u32[]{:S(2)}, u32[]{:S(2)}) async-start(f32[32,32,256]{2,1,0:T(8,128)} %broadcast_in_dim.89), calls=%async_computation.16 | async-start | bytes 2097152 | tf_op jit(solution)/shard_map/all_to_all | solution.py:34
  408.5 21.1 %all-to-all-start.17 = ((f32[32,32,256]{2,1,0:T(8,128)}), f32[32,32,256]{2,1,0:T(8,128)S(1)}, u32[]{:S(2)}, u32[]{:S(2)}) async-start(f32[32,32,256]{2,1,0:T(8,128)} %broadcast_in_dim.90), calls=%async_computation.17 | async-start | bytes 2097152 | tf_op jit(solution)/shard_map/all_to_all | solution.py:34
  412.8 16.8 %copy-start.26 = (s32[1,32]{1,0:T(1,128)S(1)}, s32[1,32]{1,0:T(1,128)}, u32[]{:S(2)}) copy-start(s32[1,32]{1,0:T(1,128)} %param.14) | copy-start | bytes 388
  432.8 1.3 copy-start.7
  434.1 10.2 %collective-permute-start.12 = (f32[1,512,256]{1,2,0:T(8,128)S(1)}, f32[1,512,256]{1,2,0:T(8,128)S(1)}, u32[]{:S(2)}, u32[]{:S(2)}) collective-permute-start(f32[1,512,256]{1,2,0:T(8,128)S(1)} %get-tuple-element.20), channel_id=1, source_target_pairs={{0,1},{1,2},{2,3},{3,4},{4,5},{5,6},{6,7},{7,8},{8,9},{9,10},{10,1... | collective-permute-start | bytes 1572872 | tf_op jit(solution)/shard_map/ppermute | solution.py:23
  436.3 15.1 %collective-permute-start.15 = (f32[1,512,256]{1,2,0:T(8,128)S(1)}, f32[1,512,256]{1,2,0:T(8,128)S(1)}, u32[]{:S(2)}, u32[]{:S(2)}) collective-permute-start(f32[1,512,256]{1,2,0:T(8,128)S(1)} %get-tuple-element.21), channel_id=1, source_target_pairs={{32,0},{64,32},{96,64},{33,1},{65,33},{97,65},{34,2},{66,34},{98,6... | collective-permute-start | bytes 1572872 | tf_op jit(solution)/shard_map/ppermute | solution.py:25
  437.6 14.7 %collective-permute-start.14 = (f32[1,512,256]{1,2,0:T(8,128)S(1)}, f32[1,512,256]{1,2,0:T(8,128)S(1)}, u32[]{:S(2)}, u32[]{:S(2)}) collective-permute-start(f32[1,512,256]{1,2,0:T(8,128)S(1)} %get-tuple-element.22), channel_id=1, source_target_pairs={{0,32},{32,64},{64,96},{1,33},{33,65},{65,97},{2,34},{34,66},{66,9... | collective-permute-start | bytes 1572872 | tf_op jit(solution)/shard_map/ppermute | solution.py:23
  441.6 10.7 %collective-permute-start.13 = (f32[1,512,256]{1,2,0:T(8,128)S(1)}, f32[1,512,256]{1,2,0:T(8,128)S(1)}, u32[]{:S(2)}, u32[]{:S(2)}) collective-permute-start(f32[1,512,256]{1,2,0:T(8,128)S(1)} %get-tuple-element.23), channel_id=1, source_target_pairs={{1,0},{2,1},{3,2},{4,3},{5,4},{6,5},{7,6},{8,7},{9,8},{10,9},{11,1... | collective-permute-start | bytes 1572872 | tf_op jit(solution)/shard_map/ppermute | solution.py:25
  479.5 3.1 copy-start.2
  482.6 25.1 %copy-start.21 = (f32[256]{0:T(256)S(1)}, f32[256]{0:T(256)}, u32[]{:S(2)}) copy-start(f32[256]{0:T(256)} %copy-done.20) | copy-start | bytes 3076
  516.1 1.5 copy-start.12
  517.6 31.1 %collective-permute-start.16 = (f32[1,512,256]{1,2,0:T(8,128)}, f32[1,512,256]{1,2,0:T(8,128)S(1)}, u32[]{:S(2)}, u32[]{:S(2)}) collective-permute-start(f32[1,512,256]{1,2,0:T(8,128)} %get-tuple-element.16), channel_id=1, source_target_pairs={{0,1},{1,2},{2,3},{3,4},{4,5},{5,6},{6,7},{7,8},{8,9},{9,10},{10,1... | collective-permute-start | bytes 1572872 | tf_op jit(solution)/shard_map/ppermute | solution.py:23
  521.4 27.3 %collective-permute-start.19 = (f32[1,512,256]{1,2,0:T(8,128)S(1)}, f32[1,512,256]{1,2,0:T(8,128)S(1)}, u32[]{:S(2)}, u32[]{:S(2)}) collective-permute-start(f32[1,512,256]{1,2,0:T(8,128)S(1)} %get-tuple-element.17), channel_id=1, source_target_pairs={{32,0},{64,32},{96,64},{33,1},{65,33},{97,65},{34,2},{66,34},{98,6... | collective-permute-start | bytes 1572872 | tf_op jit(solution)/shard_map/ppermute | solution.py:25
  522.7 26.0 %collective-permute-start.18 = (f32[1,512,256]{1,2,0:T(8,128)S(1)}, f32[1,512,256]{1,2,0:T(8,128)S(1)}, u32[]{:S(2)}, u32[]{:S(2)}) collective-permute-start(f32[1,512,256]{1,2,0:T(8,128)S(1)} %get-tuple-element.18), channel_id=1, source_target_pairs={{0,32},{32,64},{64,96},{1,33},{33,65},{65,97},{2,34},{34,66},{66,9... | collective-permute-start | bytes 1572872 | tf_op jit(solution)/shard_map/ppermute | solution.py:23
  526.7 22.0 %collective-permute-start.17 = (f32[1,512,256]{1,2,0:T(8,128)S(1)}, f32[1,512,256]{1,2,0:T(8,128)}, u32[]{:S(2)}, u32[]{:S(2)}) collective-permute-start(f32[1,512,256]{1,2,0:T(8,128)S(1)} %get-tuple-element.19), channel_id=1, source_target_pairs={{1,0},{2,1},{3,2},{4,3},{5,4},{6,5},{7,6},{8,7},{9,8},{10,9},{11,1... | collective-permute-start | bytes 1572872 | tf_op jit(solution)/shard_map/ppermute | solution.py:25
  577.1 3.1 copy-start.3
  577.1 3.1 copy-start.23
  586.8 3.0 copy-start.13
where the time goes:
time: 601 us; the launch traced here: 592 us
  local copies, waits for them, and re-layouts  169 us (28%)
  blocking collectives  168 us (28%)
  waiting for transfers between devices  89 us (15%)
  starting transfers between devices  88.5 us (15%)
  matrix products  42.7 us (7%)
  other arithmetic  33.2 us (6%)
    gather x10, local copies, waits for them, and re-layouts, assemble(): moved = jax.vmap(lambda block, order: block[order])(received, mapping)  133 us
    all_to_all x9, blocking collectives, copy_for_each(): return lax.all_to_all(copies, axis, split_axis=0, concat_axis=0, tiled=True)  83.5 us
    all_to_all x7, waiting for transfers between devices, copy_for_each(): return lax.all_to_all(copies, axis, split_axis=0, concat_axis=0, tiled=True)  65.8 us
    all_to_all x4, blocking collectives, summed_on_arrival(): blocks = lax.all_to_all(split_up(array, dim, count), axis, 0, 0, tiled=True)  55.7 us
    ppermute x10, starting transfers between devices, extended(): lax.ppermute(tail, axis, [(i, (i + 1) % count) for i in range(ends)])  37.5 us
    all_to_all x7, starting transfers between devices, copy_for_each(): return lax.all_to_all(copies, axis, split_axis=0, concat_axis=0, tiled=True)  33.2 us
    all_to_all x2, blocking collectives, sum_in_two_steps(): return jnp.sum(lax.all_to_all(own, far, 0, 0, tiled=True), axis=0)  29.1 us
    ppermute x10, starting transfers between devices, extended(): lax.ppermute(head, axis, [((i + 1) % count, i) for i in range(ends)])  17.8 us
  transfers between devices with their start and end apart: 27, of which 15 were waited for; matrix products, arithmetic and copies ran while one was open for 5% of the time, Pallas kernels for 0%

commit v1 on v0

v1 whole, which is shorter than its diff:
```python
import jax
import jax.numpy as jnp
from jax import lax
from jax.experimental import pallas as pl
from jax.experimental.pallas import tpu as pltpu
from jax.sharding import PartitionSpec as P

MESH = pl.DeviceIdType.MESH
HIGHEST = lax.Precision.HIGHEST
F32 = jnp.float32
BF16 = jnp.bfloat16

ROWS = 4
COLS = 32
IFACE = 2048
FACE = 512
RHS = 256
PRIM = 32
NQ = 128
NCG = 1024
ITERS = 2
BLOCK = NCG // COLS


def dot(a, b):
    return jnp.dot(a, b, preferred_element_type=F32)


def halves(value):
    high = value.astype(BF16)
    return high, (value - high.astype(F32)).astype(BF16)


def column_sums(value):
    return jnp.sum(value, axis=0, keepdims=True)


def eighths(value):
    return jnp.sum(value.reshape(FACE // 8, 8, RHS), axis=0)


def kernel(
    load_h, schur_h, linv_h, fmap, basis, index, ginv, lifting, cinv,
    x_out, r_out,
    sv, lv, r, t, q, zz, wb, perm, send, recv, cmat, nbsend, nbrecv,
    mysetup, srecv, gin, et, fm, whi, wlo, grc, gc,
    pbuf, xrecv, zcs, zcr, obuf, orecv, pk, pkr, red, redr, redz, redzr, acc, scal,
    load_sem, mat_sem, face_ssem, face_rsem, nb_ssem, nb_rsem, set_sem, gin_sem,
    x_sem, zc_sem, o_sem, pk_ssem, pk_rsem, red_sem, redz_sem, out_sem,
):
    g = lax.axis_index("grp")
    c = lax.axis_index("cell")
    xq = c // 8
    rest = c % 8

    def rows(f):
        return pl.ds(pl.multiple_of(f * FACE, FACE), FACE)

    def where_is(f):
        axis = f // 2
        sign = 2 * (f % 2) - 1
        gg = g + axis * sign
        cc = c + (1 - axis) * sign
        exists = jnp.logical_and(
            jnp.logical_and(gg >= 0, gg < ROWS), jnp.logical_and(cc >= 0, cc < COLS)
        )
        return exists, (gg, cc)

    def weight(f):
        exists, _ = where_is(f)
        return jnp.where(exists, 0.5, 1.0).astype(F32)

    def other(f):
        return f + 1 - 2 * (f % 2)

    load_copies = [
        pltpu.make_async_copy(
            load_h.at[pl.ds(f * FACE, FACE)], r.at[pl.ds(f * FACE, FACE)], load_sem.at[f]
        )
        for f in range(4)
    ]
    for f in (3, 2, 1, 0):
        load_copies[f].start()
    linv_copy = pltpu.make_async_copy(linv_h, lv, mat_sem.at[0])
    linv_copy.start()
    schur_copy = pltpu.make_async_copy(schur_h, sv, mat_sem.at[1])
    schur_copy.start()

    barrier = pltpu.get_barrier_semaphore()

    def greet_row(k, carry):
        pl.semaphore_signal(
            barrier, inc=1, device_id=(g, (c + k) % COLS), device_id_type=MESH
        )
        return carry

    lax.fori_loop(1, COLS, greet_row, 0)
    for k in range(1, ROWS):
        pl.semaphore_signal(
            barrier, inc=1, device_id=((g + k) % ROWS, c), device_id_type=MESH
        )

    def build_perm(f, carry):
        mine = fmap[pl.ds(f, 1), :]
        places = lax.broadcasted_iota(jnp.int32, (FACE, FACE), 0)
        perm[pl.ds(f, 1)] = jnp.where(places == mine, 1.0, 0.0).astype(BF16)[None]
        return carry

    lax.fori_loop(0, 4, build_perm, 0)
    pl.semaphore_wait(barrier, COLS - 1 + ROWS - 1)

    def face_copy(e, f):
        _, there = where_is(f)
        return pltpu.make_async_remote_copy(
            src_ref=send.at[f],
            dst_ref=recv.at[e, other(f)],
            send_sem=face_ssem.at[f],
            recv_sem=face_rsem.at[e, other(f)],
            device_id=there,
            device_id_type=MESH,
        )

    def face_arrival(e, f):
        _, there = where_is(f)
        return pltpu.make_async_remote_copy(
            src_ref=send.at[f],
            dst_ref=recv.at[e, f],
            send_sem=face_ssem.at[f],
            recv_sem=face_rsem.at[e, f],
            device_id=there,
            device_id_type=MESH,
        )

    def send_face(e, f, ref):
        exists, _ = where_is(f)

        @pl.when(exists)
        def _():
            high, low = halves(ref[rows(f)])
            order = perm[pl.ds(f, 1)].reshape(FACE, FACE)
            send[pl.ds(f, 1)] = (dot(order, high) + dot(order, low))[None]
            face_copy(e, f).start()

    def await_face(e, f):
        exists, _ = where_is(f)

        @pl.when(exists)
        def _():
            arrival = face_arrival(e, f)
            arrival.wait_recv()
            arrival.wait_send()

        @pl.when(jnp.logical_not(exists))
        def _():
            recv[pl.ds(e, 1), pl.ds(f, 1)] = jnp.zeros((1, 1, FACE, RHS), F32)

    def face_of(e, f):
        return recv[pl.ds(e, 1), pl.ds(f, 1)].reshape(FACE, RHS)

    for f in (3, 2, 1, 0):
        load_copies[f].wait()
        send_face(0, f, r)

    lane = lax.broadcasted_iota(jnp.int32, (PRIM, 128), 1)
    line = lax.broadcasted_iota(jnp.int32, (PRIM, 128), 0)
    spots = index[...].astype(F32)
    spots = jnp.broadcast_to(spots, (8, PRIM))
    low_spots = jnp.dot(
        spots, jnp.where(line == lane % 16, 1.0, 0.0).astype(F32),
        precision=HIGHEST, preferred_element_type=F32,
    )
    high_spots = jnp.dot(
        spots, jnp.where(line == lane % 16 + 16, 1.0, 0.0).astype(F32),
        precision=HIGHEST, preferred_element_type=F32,
    )
    mysetup[0:BLOCK] = lifting[...]
    mysetup[BLOCK : BLOCK + 8] = low_spots
    mysetup[BLOCK + 8 : BLOCK + 16] = high_spots
    srecv[pl.ds(c, 1)] = mysetup[...][None]

    def setup_copy(k):
        return pltpu.make_async_remote_copy(
            src_ref=mysetup,
            dst_ref=srecv.at[c],
            send_sem=set_sem.at[0],
            recv_sem=set_sem.at[1],
            device_id=(g, (c + k) % COLS),
            device_id_type=MESH,
        )

    def start_setup(k, carry):
        setup_copy(k).start()
        return carry

    lax.fori_loop(1, COLS, start_setup, 0)

    def gin_copy(k):
        return pltpu.make_async_remote_copy(
            src_ref=ginv,
            dst_ref=gin.at[xq],
            send_sem=gin_sem.at[0],
            recv_sem=gin_sem.at[1],
            device_id=(g, ((xq + k) % 4) * 8 + rest),
            device_id_type=MESH,
        )

    for k in range(1, 4):
        gin_copy(k).start()
    gin[pl.ds(xq, 1)] = ginv[...][None]

    def nb_copy(f, slot):
        _, there = where_is(f)
        return pltpu.make_async_remote_copy(
            src_ref=nbsend.at[f],
            dst_ref=nbrecv.at[slot],
            send_sem=nb_ssem.at[f],
            recv_sem=nb_rsem.at[slot],
            device_id=there,
            device_id_type=MESH,
        )

    for f in range(4):
        exists, _ = where_is(f)

        @pl.when(exists)
        def _():
            nbsend[f] = lax.dot_general(
                basis[:, f * FACE : (f + 1) * FACE], perm[f],
                (((1,), (1,)), ((), ())), preferred_element_type=F32,
            )
            nb_copy(f, f ^ 1).start()

        @pl.when(jnp.logical_not(exists))
        def _():
            nbrecv[f] = jnp.zeros((PRIM, FACE), F32)
            pkr[0, f] = jnp.zeros((PRIM, RHS), F32)
            pkr[1, f] = jnp.zeros((PRIM, RHS), F32)

    q[...] = jnp.zeros_like(q)
    scal[...] = jnp.ones_like(scal)

    def wait_bytes(ref, ssem, rsem, to):
        both = pltpu.make_async_remote_copy(
            src_ref=ref, dst_ref=ref, send_sem=ssem, recv_sem=rsem,
            device_id=to, device_id_type=MESH,
        )
        both.wait_recv()
        both.wait_send()

    row_peer = (g, (c + 1) % COLS)
    z_peer = ((g + 1) % ROWS, c)

    for f in range(4):
        exists, _ = where_is(f)

        @pl.when(exists)
        def _():
            both = nb_copy(f, f)
            both.wait_recv()
            both.wait_send()

        own = basis[:, f * FACE : (f + 1) * FACE].astype(F32)
        near = nbrecv[f]
        cmat[f] = (jnp.concatenate([own, own, near, near], axis=0) * weight(f)).T.astype(BF16)

    wait_bytes(srecv.at[pl.ds(0, COLS - 1)], set_sem.at[0], set_sem.at[1], row_peer)
    wait_bytes(gin.at[pl.ds(0, 3)], gin_sem.at[0], gin_sem.at[1], row_peer)

    lane1 = lax.broadcasted_iota(jnp.int32, (1, 128), 1)

    def spots_of(line_number):
        parts = []
        for quarter in range(4):
            total = jnp.zeros((1, 128), F32)
            for n in range(8 * quarter, 8 * quarter + 8):
                row = srecv[n, line_number : line_number + 1, :]
                total = total + jnp.where(lane1 // 16 == n % 8, row, 0.0)
            parts.append(total)
        return jnp.concatenate(parts, axis=1).astype(jnp.int32)

    wanted = jnp.concatenate([spots_of(BLOCK), spots_of(BLOCK + 8)], axis=1)

    for block in range(8):
        target = lax.broadcasted_iota(jnp.int32, (128, NCG), 0) + block * 128
        et[pl.ds(block * 128, 128)] = jnp.where(target == wanted, 1.0, 0.0).astype(BF16)

    own_row = lax.broadcasted_iota(jnp.int32, (128, NCG), 0)
    own_row = (own_row // BLOCK) * (8 * BLOCK) + rest * BLOCK + own_row % BLOCK
    fm[...] = jnp.where(own_row == wanted, 1.0, 0.0).astype(F32).T.astype(BF16)

    high, low = halves(gin[...].reshape(128, NCG))
    whi[0:128] = high
    wlo[0:128] = low
    all_lifting = srecv[:, 0:BLOCK, :].reshape(NCG, NQ)
    high, low = halves(all_lifting.T)
    whi[128:256] = high
    wlo[128:256] = low
    own_lifting = jnp.concatenate(
        [srecv[pl.ds(8 * k + rest, 1), 0:BLOCK, :].reshape(BLOCK, NQ) for k in range(4)], axis=0
    )
    grc[...] = jnp.dot(own_lifting, cinv[...], precision=HIGHEST, preferred_element_type=F32)

    linv_copy.wait()
    schur_copy.wait()

    def settle_start(i, carry):
        await_face(0, i)
        value = r[rows(i)] + face_of(0, i)
        r[rows(i)] = value
        wb[rows(i)] = (value * weight(i)).astype(BF16)
        return carry

    lax.fori_loop(0, 4, settle_start, 0)

    lane_wide = lax.broadcasted_iota(jnp.int32, (16, 128), 1)

    def left(shape):
        return lax.broadcasted_iota(jnp.int32, shape, 1) < 64

    def swap(value):
        return pltpu.roll(value, 64, 1)

    def coarse(it):
        def x_copy(k):
            there = (c + k) % COLS
            return pltpu.make_async_remote_copy(
                src_ref=pbuf.at[there // 8],
                dst_ref=xrecv.at[it, c],
                send_sem=x_sem.at[it, 0],
                recv_sem=x_sem.at[it, 1],
                device_id=(g, there),
                device_id_type=MESH,
            )

        primal = dot(basis[...], wb[...])
        for pair in range(2):
            part = primal[:, 128 * pair : 128 * pair + 128]
            top, bottom = part[0:16], part[16:32]
            pbuf[2 * pair] = jnp.where(lane_wide < 64, top, swap(bottom))
            pbuf[2 * pair + 1] = jnp.where(lane_wide < 64, swap(top), bottom)

        def start(k, carry):
            x_copy(k).start()
            return carry

        lax.fori_loop(1, COLS, start, 0)
        xrecv[pl.ds(it, 1), pl.ds(c, 1)] = pbuf[pl.ds(xq, 1)][None]

    def solve_coarse(it):
        wait_bytes(xrecv.at[it, pl.ds(0, COLS - 1)], x_sem.at[it, 0], x_sem.at[it, 1], row_peer)
        block = xrecv[pl.ds(it, 1)].reshape(FACE, 128)
        parts = jnp.concatenate(halves(block), axis=1)
        upper = dot(et[:, 0:512], parts)
        lower = dot(et[:, 512:1024], parts)
        upper = upper[:, 0:128] + upper[:, 128:256]
        lower = lower[:, 0:128] + lower[:, 128:256]
        gc[...] = upper + swap(lower)
        high, low = halves(gc[...])
        both = dot(whi[...], jnp.concatenate([high, low], axis=1))
        both = both[:, 0:128] + both[:, 128:256] + dot(wlo[...], high)
        from_row = both[0:128]
        partial = both[128:256]
        packed = jnp.where(left((64, 128)), partial[0:64], swap(partial[64:128]))
        zcs[...] = packed
        zcr[pl.ds(it, 1), pl.ds(g, 1)] = packed[None, None]

        def z_copy(k):
            return pltpu.make_async_remote_copy(
                src_ref=zcs,
                dst_ref=zcr.at[it, g],
                send_sem=zc_sem.at[it, 0],
                recv_sem=zc_sem.at[it, 1],
                device_id=((g + k) % ROWS, c),
                device_id_type=MESH,
            )

        for k in range(1, ROWS):
            z_copy(k).start()
        wait_bytes(zcr.at[it, pl.ds(0, ROWS - 1)], zc_sem.at[it, 0], zc_sem.at[it, 1], z_peer)
        blocks = zcr[pl.ds(it, 1)].reshape(ROWS, 64, 128)
        total = (blocks[0] + blocks[1]) + (blocks[2] + blocks[3])
        coarsest = jnp.concatenate([total, swap(total)], axis=0)
        owned = from_row + jnp.dot(
            grc[...], coarsest, precision=HIGHEST, preferred_element_type=F32
        )
        parts = jnp.concatenate(halves(owned), axis=1)
        back = dot(fm[...], parts)
        back = back[:, 0:128] + back[:, 128:256]
        packed = jnp.where(left((FACE, 128)), back[0:512], swap(back[512:1024]))
        obuf[...] = packed.reshape(COLS, 16, 128)

        def o_copy(k):
            there = (c + k) % COLS
            return pltpu.make_async_remote_copy(
                src_ref=obuf.at[there],
                dst_ref=orecv.at[it, c],
                send_sem=o_sem.at[it, 0],
                recv_sem=o_sem.at[it, 1],
                device_id=(g, there),
                device_id_type=MESH,
            )

        def start(k, carry):
            o_copy(k).start()
            return carry

        lax.fori_loop(1, COLS, start, 0)
        orecv[pl.ds(it, 1), pl.ds(c, 1)] = obuf[pl.ds(c, 1)][None]
        wait_bytes(orecv.at[it, pl.ds(0, COLS - 1)], o_sem.at[it, 0], o_sem.at[it, 1], row_peer)
        arrived = orecv[pl.ds(it, 1)].reshape(4, 8, 16, 128)
        sums = jnp.sum(arrived, axis=1)
        columns = []
        for pair in range(2):
            first, second = sums[2 * pair], sums[2 * pair + 1]
            top = jnp.where(lane_wide < 64, first, swap(second))
            bottom = jnp.where(lane_wide < 64, swap(first), second)
            columns.append(jnp.concatenate([top, bottom], axis=0))
        pk[...] = jnp.concatenate(columns, axis=1)

        def pk_copy(f, slot):
            _, there = where_is(f)
            return pltpu.make_async_remote_copy(
                src_ref=pk,
                dst_ref=pkr.at[it, slot],
                send_sem=pk_ssem.at[f],
                recv_sem=pk_rsem.at[it, slot],
                device_id=there,
                device_id_type=MESH,
            )

        for f in range(4):
            exists, _ = where_is(f)

            @pl.when(exists)
            def _():
                pk_copy(f, f ^ 1).start()

        for f in range(4):
            exists, _ = where_is(f)

            @pl.when(exists)
            def _():
                arrival = pk_copy(f, f)
                arrival.wait_recv()
                arrival.wait_send()

    def step(it, carry):
        acc[...] = jnp.zeros_like(acc)
        first = 1 + 2 * it
        second = 2 + 2 * it

        coarse(it)

        def local(i, carry):
            f = 3 - i
            t[rows(f)] = dot(lv[rows(f)], wb[...]) * weight(f)
            send_face(first, f, t)
            return carry

        lax.fori_loop(0, 4, local, 0)
        solve_coarse(it)
        own_high, own_low = halves(pk[...])

        def settle(f, carry):
            await_face(first, f)
            near_high, near_low = halves(
                pkr[pl.ds(it, 1), pl.ds(f, 1)].reshape(PRIM, RHS)
            )
            stack = jnp.concatenate([own_high, own_low, near_high, near_low], axis=0)
            rank = dot(cmat[pl.ds(f, 1)].reshape(FACE, 128), stack)
            value = t[rows(f)] + face_of(first, f) + rank
            zz[pl.ds(it, 1), rows(f)] = value[None]
            wide = weight(f)
            acc[0] += wide * eighths(value * r[rows(f)])
            acc[1] += wide * eighths(value * q[rows(f)])
            return carry

        lax.fori_loop(0, 4, settle, 0)

        def narrow(f, carry):
            wb[rows(f)] = zz[pl.ds(it, 1), rows(f)].reshape(FACE, RHS).astype(BF16)
            return carry

        lax.fori_loop(0, 4, narrow, 0)

        def stiff(i, carry):
            f = 3 - i
            value = dot(sv[rows(f)], wb[...])
            t[rows(f)] = value
            send_face(second, f, t)
            acc[2] += eighths(value * zz[pl.ds(it, 1), rows(f)].reshape(FACE, RHS))
            acc[3] += eighths(value * zz[0, rows(f)])
            return carry

        lax.fori_loop(0, 4, stiff, 0)
        red[...] = jnp.zeros_like(red)
        for k in range(4):
            red[k : k + 1] = column_sums(acc[k])

        def red_copy(k):
            return pltpu.make_async_remote_copy(
                src_ref=red,
                dst_ref=redr.at[it, c],
                send_sem=red_sem.at[it, 0],
                recv_sem=red_sem.at[it, 1],
                device_id=(g, (c + k) % COLS),
                device_id_type=MESH,
            )

        def start(k, carry):
            red_copy(k).start()
            return carry

        lax.fori_loop(1, COLS, start, 0)
        redr[pl.ds(it, 1), pl.ds(c, 1)] = red[...][None, None]
        wait_bytes(
            redr.at[it, pl.ds(0, COLS - 1)], red_sem.at[it, 0], red_sem.at[it, 1], row_peer
        )
        row_sum = jnp.sum(redr[pl.ds(it, 1)].reshape(COLS, 8, RHS), axis=0)
        redz[...] = row_sum
        redzr[pl.ds(it, 1), pl.ds(g, 1)] = row_sum[None, None]

        def redz_copy(k):
            return pltpu.make_async_remote_copy(
                src_ref=redz,
                dst_ref=redzr.at[it, g],
                send_sem=redz_sem.at[it, 0],
                recv_sem=redz_sem.at[it, 1],
                device_id=((g + k) % ROWS, c),
                device_id_type=MESH,
            )

        for k in range(1, ROWS):
            redz_copy(k).start()
        wait_bytes(
            redzr.at[it, pl.ds(0, ROWS - 1)], redz_sem.at[it, 0], redz_sem.at[it, 1], z_peer
        )
        sums = jnp.sum(redzr[pl.ds(it, 1)].reshape(ROWS, 8, RHS), axis=0)
        rz = sums[0:1]
        beta = jnp.where(it > 0, rz / scal[0:1], 0.0)
        curv = sums[2:3] + beta * (sums[1:2] + sums[3:4]) + beta * beta * scal[1:2]
        alpha = rz / curv
        scal[3:4] = scal[2:3]
        scal[0:1] = rz
        scal[1:2] = curv
        scal[2:3] = alpha
        scal[4:5] = beta

        def update(f, carry):
            await_face(second, f)
            image = t[rows(f)] + face_of(second, f) + beta * q[rows(f)]
            q[rows(f)] = image
            value = r[rows(f)] - alpha * image
            r[rows(f)] = value
            wb[rows(f)] = (value * weight(f)).astype(BF16)
            return carry

        lax.fori_loop(0, 4, update, 0)
        return carry

    lax.fori_loop(0, ITERS, step, 0)
    alpha = scal[2:3]
    held = scal[3:4] + alpha * scal[4:5]

    def finish(f, carry):
        t[rows(f)] = held * zz[0, rows(f)] + alpha * zz[1, rows(f)]
        return carry

    r_copy = pltpu.make_async_copy(r, r_out, out_sem.at[0])
    r_copy.start()
    lax.fori_loop(0, 4, finish, 0)
    x_copy = pltpu.make_async_copy(t, x_out, out_sem.at[1])
    x_copy.start()
    r_copy.wait()
    x_copy.wait()


def body(
    load, schur, local_inverse, face_map, primal_basis, primal_index,
    group_inverse, group_to_coarsest, coarsest_inverse,
):
    anywhere = pl.BlockSpec(memory_space=pl.ANY)
    near = pl.BlockSpec(memory_space=pltpu.VMEM)
    dma = pltpu.SemaphoreType.DMA
    out = jax.ShapeDtypeStruct((IFACE, RHS), F32)
    x, r = pl.pallas_call(
        kernel,
        out_shape=(out, out),
        in_specs=[anywhere] * 3 + [near] * 6,
        out_specs=(anywhere, anywhere),
        scratch_shapes=[
            pltpu.VMEM((IFACE, IFACE), BF16),
            pltpu.VMEM((IFACE, IFACE), BF16),
            pltpu.VMEM((IFACE, RHS), F32),
            pltpu.VMEM((IFACE, RHS), F32),
            pltpu.VMEM((IFACE, RHS), F32),
            pltpu.VMEM((ITERS, IFACE, RHS), F32),
            pltpu.VMEM((IFACE, RHS), BF16),
            pltpu.VMEM((4, FACE, FACE), BF16),
            pltpu.VMEM((4, FACE, RHS), F32),
            pltpu.VMEM((1 + 2 * ITERS, 4, FACE, RHS), F32),
            pltpu.VMEM((4, FACE, 128), BF16),
            pltpu.VMEM((4, PRIM, FACE), F32),
            pltpu.VMEM((4, PRIM, FACE), F32),
            pltpu.VMEM((BLOCK + 16, NQ), F32),
            pltpu.VMEM((COLS, BLOCK + 16, NQ), F32),
            pltpu.VMEM((4, BLOCK, NCG), F32),
            pltpu.VMEM((NCG, NCG), BF16),
            pltpu.VMEM((NCG, 128), BF16),
            pltpu.VMEM((256, NCG), BF16),
            pltpu.VMEM((256, NCG), BF16),
            pltpu.VMEM((128, NQ), F32),
            pltpu.VMEM((NCG, 128), F32),
            pltpu.VMEM((4, 16, 128), F32),
            pltpu.VMEM((ITERS, COLS, 16, 128), F32),
            pltpu.VMEM((64, 128), F32),
            pltpu.VMEM((ITERS, ROWS, 64, 128), F32),
            pltpu.VMEM((COLS, 16, 128), F32),
            pltpu.VMEM((ITERS, COLS, 16, 128), F32),
            pltpu.VMEM((PRIM, RHS), F32),
            pltpu.VMEM((ITERS, 4, PRIM, RHS), F32),
            pltpu.VMEM((8, RHS), F32),
            pltpu.VMEM((ITERS, COLS, 8, RHS), F32),
            pltpu.VMEM((8, RHS), F32),
            pltpu.VMEM((ITERS, ROWS, 8, RHS), F32),
            pltpu.VMEM((4, 8, RHS), F32),
            pltpu.VMEM((8, RHS), F32),
            dma((4,)), dma((2,)), dma((4,)), dma((1 + 2 * ITERS, 4)),
            dma((4,)), dma((4,)), dma((2,)), dma((2,)),
            dma((ITERS, 2)), dma((ITERS, 2)), dma((ITERS, 2)),
            dma((4,)), dma((ITERS, 4)), dma((ITERS, 2)), dma((ITERS, 2)), dma((2,)),
        ],
        compiler_params=pltpu.CompilerParams(
            collective_id=0, has_side_effects=True, vmem_limit_bytes=63 * 1024 * 1024
        ),
    )(
        load[0], schur[0], local_inverse[0], face_map[0], primal_basis[0], primal_index,
        group_inverse[0], group_to_coarsest[0], coarsest_inverse,
    )
    return x[None], r[None]


def solution(mesh):
    spread = ("grp", "cell")
    in_specs = (
        P(spread, None, None),
        P(spread, None, None),
        P(spread, None, None),
        P(spread, None, None),
        P(spread, None, None),
        P(spread, None),
        P("grp", "cell", None),
        P("grp", "cell", None),
        P(),
    )
    out_specs = (P(spread, None, None), P(spread, None, None))
    return jax.shard_map(body, mesh=mesh, in_specs=in_specs, out_specs=out_specs, check_vma=False)
```

time: 601 us -> 141 us (0.23); the launches traced: 592 us -> 141 us
  blocking collectives: 168 us -> 0 us
  local copies, waits for them, and re-layouts: 169 us -> 4.52 us
  Pallas kernels: 0 us -> 136 us
  waiting for transfers between devices: 89 us -> 0 us
  starting transfers between devices: 88.5 us -> 0 us
  matrix products: 42.7 us -> 0 us
  other arithmetic: 33.2 us -> 0 us
    all_to_all x15 -> x0, blocking collectives: 168 us -> none  [the longest x9 83.5 us: copy_for_each(): return lax.all_to_all(copies, axis, split_axis=0, concat_axis=0, tiled=True)]
    pallas_call x0 -> x1, Pallas kernels: none -> 136 us  [body(): pl.pallas_call(kernel, out_shape=(out, out), in_specs=[anywhere] * 3 + [n...]
    gather x10 -> x0, local copies, waits for them, and re-layouts: 133 us -> none  [assemble(): moved = jax.vmap(lambda block, order: block[order])(received, mapping)]
    all_to_all x7 -> x0, waiting for transfers between devices: 65.8 us -> none  [copy_for_each(): return lax.all_to_all(copies, axis, split_axis=0, concat_axis=0, tiled=True)]
    ppermute x20 -> x0, starting transfers between devices: 55.3 us -> none  [the longest x10 37.5 us: extended(): lax.ppermute(tail, axis, [(i, (i + 1) % count) for i in range(ends)])]
    dot_general x20 -> x0, matrix products: 42.7 us -> none  [the longest x2 15.1 us: body(): jnp.dot(matrix, direction.astype(jnp.bfloat16), preferred_element_type=jn...]
    all_to_all x7 -> x0, starting transfers between devices: 33.2 us -> none  [copy_for_each(): return lax.all_to_all(copies, axis, split_axis=0, concat_axis=0, tiled=True)]
    ppermute x20 -> x0, waiting for transfers between devices: 23.2 us -> none  [the longest x10 14 us: extended(): lax.ppermute(head, axis, [((i + 1) % count, i) for i in range(ends)])]
  transfers between devices with their start and end apart: 27 -> 0, of which waited for: 15 -> 0; matrix products, arithmetic and copies ran while one was open for 5% -> 0% of each run, Pallas kernels for 0% -> 0%
where the time goes in v1:
time: 141 us
  Pallas kernels  136 us (96%)
  local copies, waits for them, and re-layouts  4.52 us (3%)
    pallas_call x1, Pallas kernels, body(): pl.pallas_call(kernel, out_shape=(out, out), in_specs=[anywhere] * 3 + [n...  136 us
    unnamed x4, local copies, waits for them, and re-layouts  4.52 us

profile of v1, /device:TPU:1, one launch (start us, length us, event | category | flops | bytes accessed | tf_op | source)
XLA Modules:
  0.0 141.2 jit_solution(12743114053858348162)
XLA Ops:
  0.6 136.0 %shard_map.104 = (f32[2048,256]{1,0:T(8,128)}, f32[2048,256]{1,0:T(8,128)}) custom-call(f32[2048,256]{1,0:T(8,128)} %bitcast.11, bf16[2048,2048]{1,0:T(8,128)(2,1)} %bitcast.9, bf16[2048,2048]{1,0:T(8,128)(2,1)} %bitcast.10, s32[4,512]{1,0:T(4,128)} %bitcast.17, bf16[32,2048]{1,0:T(8,128)(2,1)} %bitcast.14, s32[1,32]{1,0:T(1,128)} %index.1, ...), custom_call_target="tpu_custom_call" | custom-call | tf_op jit(solution)/shard_map/pallas_call | solution.py:586
  136.7 0.0 copy-start
  136.7 3.2 %copy.13 = f32[1,2048,256]{2,1,0:T(8,128)} copy(f32[1,2048,256]{2,1,0:T(8,128)} %bitcast.13) | data formatting | bytes 4194304
  139.9 0.0 copy-done
  139.9 1.3 copy.14
Async XLA Ops:
  136.7 3.2 %copy-start = (f32[2048,256]{1,0:T(8,128)S(1)}, f32[2048,256]{1,0:T(8,128)}, u32[]{:S(2)}) copy-start(f32[2048,256]{1,0:T(8,128)} %get-tuple-element.5) | copy-start | bytes 6291460

commit v2 on v1

--- a/solution.py
+++ b/solution.py
@@ -20,6 +20,10 @@
 NCG = 1024
 ITERS = 2
 BLOCK = NCG // COLS
+CUT_LOCAL = 384
+CUT_AGAIN = 128
+CUT_STIFF = 128
+CUT_SIDE = 256
 
 
 def dot(a, b):
@@ -43,10 +47,11 @@
     load_h, schur_h, linv_h, fmap, basis, index, ginv, lifting, cinv,
     x_out, r_out,
     sv, lv, r, t, q, zz, wb, perm, send, recv, cmat, nbsend, nbrecv,
-    mysetup, srecv, gin, et, fm, whi, wlo, grc, gc,
+    myspots, prow, srecv, gin, et, fm, whi, wlo, egc, gc, chat, sc, css, csr, pkhl,
     pbuf, xrecv, zcs, zcr, obuf, orecv, pk, pkr, red, redr, redz, redzr, acc, scal,
-    load_sem, mat_sem, face_ssem, face_rsem, nb_ssem, nb_rsem, set_sem, gin_sem,
-    x_sem, zc_sem, o_sem, pk_ssem, pk_rsem, red_sem, redz_sem, out_sem,
+    pmat, ems, emr, pq, pkb,
+    load_sem, mat_sem, face_ssem, face_rsem, nb_ssem, nb_rsem, spot_sem, set_sem, gin_sem,
+    x_sem, zc_sem, cs_sem, o_sem, pk_ssem, pk_rsem, red_sem, redz_sem, out_sem, em_ssem, em_rsem,
 ):
     g = lax.axis_index("grp")
     c = lax.axis_index("cell")
@@ -82,9 +87,7 @@
     for f in (3, 2, 1, 0):
         load_copies[f].start()
     linv_copy = pltpu.make_async_copy(linv_h, lv, mat_sem.at[0])
-    linv_copy.start()
     schur_copy = pltpu.make_async_copy(schur_h, sv, mat_sem.at[1])
-    schur_copy.start()
 
     barrier = pltpu.get_barrier_semaphore()
 
@@ -107,13 +110,12 @@
         return carry
 
     lax.fori_loop(0, 4, build_perm, 0)
-    pl.semaphore_wait(barrier, COLS - 1 + ROWS - 1)
-
-    def face_copy(e, f):
+
+    def face_copy(e, f, start, stop):
         _, there = where_is(f)
         return pltpu.make_async_remote_copy(
-            src_ref=send.at[f],
-            dst_ref=recv.at[e, other(f)],
+            src_ref=send.at[f, pl.ds(start, stop - start)],
+            dst_ref=recv.at[e, other(f), pl.ds(start, stop - start)],
             send_sem=face_ssem.at[f],
             recv_sem=face_rsem.at[e, other(f)],
             device_id=there,
@@ -131,7 +133,7 @@
             device_id_type=MESH,
         )
 
-    def send_face(e, f, ref):
+    def order_face(f, ref):
         exists, _ = where_is(f)
 
         @pl.when(exists)
@@ -139,7 +141,13 @@
             high, low = halves(ref[rows(f)])
             order = perm[pl.ds(f, 1)].reshape(FACE, FACE)
             send[pl.ds(f, 1)] = (dot(order, high) + dot(order, low))[None]
-            face_copy(e, f).start()
+
+    def start_face(e, f, start, stop):
+        exists, _ = where_is(f)
+
+        @pl.when(exists)
+        def _():
+            face_copy(e, f, start, stop).start()
 
     def await_face(e, f):
         exists, _ = where_is(f)
@@ -159,12 +167,14 @@
 
     for f in (3, 2, 1, 0):
         load_copies[f].wait()
-        send_face(0, f, r)
+        if f == 3:
+            linv_copy.start()
+            schur_copy.start()
+        order_face(f, r)
 
     lane = lax.broadcasted_iota(jnp.int32, (PRIM, 128), 1)
     line = lax.broadcasted_iota(jnp.int32, (PRIM, 128), 0)
-    spots = index[...].astype(F32)
-    spots = jnp.broadcast_to(spots, (8, PRIM))
+    spots = jnp.broadcast_to(index[...].astype(F32), (8, PRIM))
     low_spots = jnp.dot(
         spots, jnp.where(line == lane % 16, 1.0, 0.0).astype(F32),
         precision=HIGHEST, preferred_element_type=F32,
@@ -173,14 +183,37 @@
         spots, jnp.where(line == lane % 16 + 16, 1.0, 0.0).astype(F32),
         precision=HIGHEST, preferred_element_type=F32,
     )
-    mysetup[0:BLOCK] = lifting[...]
-    mysetup[BLOCK : BLOCK + 8] = low_spots
-    mysetup[BLOCK + 8 : BLOCK + 16] = high_spots
-    srecv[pl.ds(c, 1)] = mysetup[...][None]
+    first_line = lax.broadcasted_iota(jnp.int32, (8, 128), 0) == 0
+    myspots[...] = jnp.where(first_line, low_spots, high_spots)
+    prow[pl.ds(c, 1)] = myspots[...][None]
+    srecv[pl.ds(c, 1)] = lifting[...][None]
+    gin[pl.ds(xq, 1)] = ginv[...][None]
+
+    pl.semaphore_wait(barrier, COLS - 1 + ROWS - 1)
+    start_face(0, 3, 0, FACE)
+    start_face(0, 2, 0, FACE)
+
+    def spots_copy(k):
+        return pltpu.make_async_remote_copy(
+            src_ref=myspots,
+            dst_ref=prow.at[c],
+            send_sem=spot_sem.at[0],
+            recv_sem=spot_sem.at[1],
+            device_id=(g, (c + k) % COLS),
+            device_id_type=MESH,
+        )
+
+    def start_spots(k, carry):
+        spots_copy(k).start()
+        return carry
+
+    lax.fori_loop(1, COLS, start_spots, 0)
+    start_face(0, 1, 0, FACE)
+    start_face(0, 0, 0, FACE)
 
     def setup_copy(k):
         return pltpu.make_async_remote_copy(
-            src_ref=mysetup,
+            src_ref=lifting,
             dst_ref=srecv.at[c],
             send_sem=set_sem.at[0],
             recv_sem=set_sem.at[1],
@@ -191,8 +224,6 @@
     def start_setup(k, carry):
         setup_copy(k).start()
         return carry
-
-    lax.fori_loop(1, COLS, start_setup, 0)
 
     def gin_copy(k):
         return pltpu.make_async_remote_copy(
@@ -206,7 +237,7 @@
 
     for k in range(1, 4):
         gin_copy(k).start()
-    gin[pl.ds(xq, 1)] = ginv[...][None]
+    lax.fori_loop(1, COLS, start_setup, 0)
 
     def nb_copy(f, slot):
         _, there = where_is(f)
@@ -235,6 +266,7 @@
             nbrecv[f] = jnp.zeros((PRIM, FACE), F32)
             pkr[0, f] = jnp.zeros((PRIM, RHS), F32)
             pkr[1, f] = jnp.zeros((PRIM, RHS), F32)
+            emr[f] = jnp.zeros((PRIM, RHS), F32)
 
     q[...] = jnp.zeros_like(q)
     scal[...] = jnp.ones_like(scal)
@@ -250,21 +282,7 @@
     row_peer = (g, (c + 1) % COLS)
     z_peer = ((g + 1) % ROWS, c)
 
-    for f in range(4):
-        exists, _ = where_is(f)
-
-        @pl.when(exists)
-        def _():
-            both = nb_copy(f, f)
-            both.wait_recv()
-            both.wait_send()
-
-        own = basis[:, f * FACE : (f + 1) * FACE].astype(F32)
-        near = nbrecv[f]
-        cmat[f] = (jnp.concatenate([own, own, near, near], axis=0) * weight(f)).T.astype(BF16)
-
-    wait_bytes(srecv.at[pl.ds(0, COLS - 1)], set_sem.at[0], set_sem.at[1], row_peer)
-    wait_bytes(gin.at[pl.ds(0, 3)], gin_sem.at[0], gin_sem.at[1], row_peer)
+    wait_bytes(prow.at[pl.ds(0, COLS - 1)], spot_sem.at[0], spot_sem.at[1], row_peer)
 
     lane1 = lax.broadcasted_iota(jnp.int32, (1, 128), 1)
 
@@ -273,12 +291,12 @@
         for quarter in range(4):
             total = jnp.zeros((1, 128), F32)
             for n in range(8 * quarter, 8 * quarter + 8):
-                row = srecv[n, line_number : line_number + 1, :]
+                row = prow[n, line_number : line_number + 1, :]
                 total = total + jnp.where(lane1 // 16 == n % 8, row, 0.0)
             parts.append(total)
         return jnp.concatenate(parts, axis=1).astype(jnp.int32)
 
-    wanted = jnp.concatenate([spots_of(BLOCK), spots_of(BLOCK + 8)], axis=1)
+    wanted = jnp.concatenate([spots_of(0), spots_of(1)], axis=1)
 
     for block in range(8):
         target = lax.broadcasted_iota(jnp.int32, (128, NCG), 0) + block * 128
@@ -288,17 +306,54 @@
     own_row = (own_row // BLOCK) * (8 * BLOCK) + rest * BLOCK + own_row % BLOCK
     fm[...] = jnp.where(own_row == wanted, 1.0, 0.0).astype(F32).T.astype(BF16)
 
+    wait_bytes(gin.at[pl.ds(0, 3)], gin_sem.at[0], gin_sem.at[1], row_peer)
     high, low = halves(gin[...].reshape(128, NCG))
     whi[0:128] = high
     wlo[0:128] = low
-    all_lifting = srecv[:, 0:BLOCK, :].reshape(NCG, NQ)
-    high, low = halves(all_lifting.T)
-    whi[128:256] = high
-    wlo[128:256] = low
-    own_lifting = jnp.concatenate(
-        [srecv[pl.ds(8 * k + rest, 1), 0:BLOCK, :].reshape(BLOCK, NQ) for k in range(4)], axis=0
-    )
-    grc[...] = jnp.dot(own_lifting, cinv[...], precision=HIGHEST, preferred_element_type=F32)
+
+    def build_late():
+        wait_bytes(srecv.at[pl.ds(0, COLS - 1)], set_sem.at[0], set_sem.at[1], row_peer)
+        all_lifting = srecv[...].reshape(NCG, NQ)
+        high, low = halves(all_lifting.T)
+        whi[128:256] = high
+        wlo[128:256] = low
+        mine = jnp.where(lane1 < 16, myspots[0:1], myspots[1:2]).astype(jnp.int32)
+        target = lax.broadcasted_iota(jnp.int32, (NCG, 128), 0)
+        chosen = jnp.where(target == mine, 1.0, 0.0).astype(F32).T[0:PRIM].astype(BF16)
+        high, low = halves(all_lifting)
+        egc[...] = jnp.dot(
+            dot(chosen, high) + dot(chosen, low), cinv[...],
+            precision=HIGHEST, preferred_element_type=F32,
+        )
+
+    def build_rank():
+        for f in range(4):
+            exists, _ = where_is(f)
+
+            @pl.when(exists)
+            def _():
+                both = nb_copy(f, f)
+                both.wait_recv()
+                both.wait_send()
+
+            own = basis[:, f * FACE : (f + 1) * FACE].astype(F32)
+            near = nbrecv[f]
+            stack = jnp.concatenate([own, own, near, near], axis=0) * weight(f)
+            cmat[f] = stack.T.astype(BF16)
+            pmat[f] = (jnp.concatenate([own, near], axis=0) * weight(f)).astype(BF16)
+            empty = jnp.zeros((PRIM, FACE), F32)
+            stack = jnp.concatenate(
+                [own] + [near if k == f else empty for k in range(4)] + [empty] * 3, axis=0
+            )
+            chat[f * FACE : (f + 1) * FACE] = (stack * weight(f)).T.astype(BF16)
+
+        def build_images(f, carry):
+            high, low = halves(dot(sv[rows(f)], chat[...]))
+            sc[rows(f), 0:256] = high
+            sc[rows(f), 256:512] = low
+            return carry
+
+        lax.fori_loop(0, 4, build_images, 0)
 
     linv_copy.wait()
     schur_copy.wait()
@@ -320,7 +375,7 @@
     def swap(value):
         return pltpu.roll(value, 64, 1)
 
-    def coarse(it):
+    def coarse(it, primal):
         def x_copy(k):
             there = (c + k) % COLS
             return pltpu.make_async_remote_copy(
@@ -332,7 +387,6 @@
                 device_id_type=MESH,
             )
 
-        primal = dot(basis[...], wb[...])
         for pair in range(2):
             part = primal[:, 128 * pair : 128 * pair + 128]
             top, bottom = part[0:16], part[16:32]
@@ -346,7 +400,17 @@
         lax.fori_loop(1, COLS, start, 0)
         xrecv[pl.ds(it, 1), pl.ds(c, 1)] = pbuf[pl.ds(xq, 1)][None]
 
-    def solve_coarse(it):
+    def unpack(blocks, half):
+        columns = []
+        lanes = left((half, 128))
+        for pair in range(2):
+            first, second = blocks[2 * pair], blocks[2 * pair + 1]
+            top = jnp.where(lanes, first, swap(second))
+            bottom = jnp.where(lanes, swap(first), second)
+            columns.append(jnp.concatenate([top, bottom], axis=0))
+        return jnp.concatenate(columns, axis=1)
+
+    def solve_row(it, cut):
         wait_bytes(xrecv.at[it, pl.ds(0, COLS - 1)], x_sem.at[it, 0], x_sem.at[it, 1], row_peer)
         block = xrecv[pl.ds(it, 1)].reshape(FACE, 128)
         parts = jnp.concatenate(halves(block), axis=1)
@@ -358,7 +422,6 @@
         high, low = halves(gc[...])
         both = dot(whi[...], jnp.concatenate([high, low], axis=1))
         both = both[:, 0:128] + both[:, 128:256] + dot(wlo[...], high)
-        from_row = both[0:128]
         partial = both[128:256]
         packed = jnp.where(left((64, 128)), partial[0:64], swap(partial[64:128]))
         zcs[...] = packed
@@ -376,14 +439,9 @@
 
         for k in range(1, ROWS):
             z_copy(k).start()
-        wait_bytes(zcr.at[it, pl.ds(0, ROWS - 1)], zc_sem.at[it, 0], zc_sem.at[it, 1], z_peer)
-        blocks = zcr[pl.ds(it, 1)].reshape(ROWS, 64, 128)
-        total = (blocks[0] + blocks[1]) + (blocks[2] + blocks[3])
-        coarsest = jnp.concatenate([total, swap(total)], axis=0)
-        owned = from_row + jnp.dot(
-            grc[...], coarsest, precision=HIGHEST, preferred_element_type=F32
-        )
-        parts = jnp.concatenate(halves(owned), axis=1)
+        start_face(1 + 2 * it, 3, cut, FACE)
+        start_face(1 + 2 * it, 2, cut, FACE)
+        parts = jnp.concatenate(halves(both[0:128]), axis=1)
         back = dot(fm[...], parts)
         back = back[:, 0:128] + back[:, 128:256]
         packed = jnp.where(left((FACE, 128)), back[0:512], swap(back[512:1024]))
@@ -406,96 +464,241 @@
 
         lax.fori_loop(1, COLS, start, 0)
         orecv[pl.ds(it, 1), pl.ds(c, 1)] = obuf[pl.ds(c, 1)][None]
+
+    def solve_coarsest(it):
+        wait_bytes(zcr.at[it, pl.ds(0, ROWS - 1)], zc_sem.at[it, 0], zc_sem.at[it, 1], z_peer)
+        blocks = zcr[pl.ds(it, 1)].reshape(ROWS, 64, 128)
+        total = (blocks[0] + blocks[1]) + (blocks[2] + blocks[3])
+        css[...] = total
+        csr[pl.ds(it, 1), pl.ds(xq, 1)] = total[None, None]
+
+        def cs_copy(k):
+            return pltpu.make_async_remote_copy(
+                src_ref=css,
+                dst_ref=csr.at[it, xq],
+                send_sem=cs_sem.at[it, 0],
+                recv_sem=cs_sem.at[it, 1],
+                device_id=(g, ((xq + k) % 4) * 8 + rest),
+                device_id_type=MESH,
+            )
+
+        for k in range(1, 4):
+            cs_copy(k).start()
+
+    def pk_copy(it, f, slot):
+        _, there = where_is(f)
+        return pltpu.make_async_remote_copy(
+            src_ref=pk,
+            dst_ref=pkr.at[it, slot],
+            send_sem=pk_ssem.at[f],
+            recv_sem=pk_rsem.at[it, slot],
+            device_id=there,
+            device_id_type=MESH,
+        )
+
+    def pick(it):
+        wait_bytes(csr.at[it, pl.ds(0, 3)], cs_sem.at[it, 0], cs_sem.at[it, 1], row_peer)
+        coarsest = unpack([csr[it, k] for k in range(4)], 64)
         wait_bytes(orecv.at[it, pl.ds(0, COLS - 1)], o_sem.at[it, 0], o_sem.at[it, 1], row_peer)
-        arrived = orecv[pl.ds(it, 1)].reshape(4, 8, 16, 128)
-        sums = jnp.sum(arrived, axis=1)
-        columns = []
-        for pair in range(2):
-            first, second = sums[2 * pair], sums[2 * pair + 1]
-            top = jnp.where(lane_wide < 64, first, swap(second))
-            bottom = jnp.where(lane_wide < 64, swap(first), second)
-            columns.append(jnp.concatenate([top, bottom], axis=0))
-        pk[...] = jnp.concatenate(columns, axis=1)
-
-        def pk_copy(f, slot):
-            _, there = where_is(f)
-            return pltpu.make_async_remote_copy(
-                src_ref=pk,
-                dst_ref=pkr.at[it, slot],
-                send_sem=pk_ssem.at[f],
-                recv_sem=pk_rsem.at[it, slot],
-                device_id=there,
-                device_id_type=MESH,
-            )
+        sums = jnp.sum(orecv[pl.ds(it, 1)].reshape(4, 8, 16, 128), axis=1)
+        found = unpack([sums[k] for k in range(4)], 16) + jnp.dot(
+            egc[...], coarsest, precision=HIGHEST, preferred_element_type=F32
+        )
+
+        @pl.when(it == 0)
+        def _():
+            pk[...] = found
+            pkb[...] = found
+
+        @pl.when(it > 0)
+        def _():
+            pk[...] = pkb[...] - scal[2:3] * found
 
         for f in range(4):
             exists, _ = where_is(f)
 
             @pl.when(exists)
             def _():
-                pk_copy(f, f ^ 1).start()
-
+                pk_copy(it, f, f ^ 1).start()
+
+    def await_picks(it):
         for f in range(4):
             exists, _ = where_is(f)
 
             @pl.when(exists)
             def _():
-                arrival = pk_copy(f, f)
+                arrival = pk_copy(it, f, f)
                 arrival.wait_recv()
                 arrival.wait_send()
+
+    def em_copy(f, slot):
+        _, there = where_is(f)
+        return pltpu.make_async_remote_copy(
+            src_ref=ems.at[f],
+            dst_ref=emr.at[slot],
+            send_sem=em_ssem.at[f],
+            recv_sem=em_rsem.at[slot],
+            device_id=there,
+            device_id_type=MESH,
+        )
+
+    def early_send():
+        pq[...] = jnp.zeros_like(pq)
+
+        def one(i, carry):
+            f = 3 - i
+            both = dot(pmat[pl.ds(f, 1)].reshape(2 * PRIM, FACE), jnp.concatenate(
+                halves(t[rows(f)]), axis=1
+            ))
+            both = both[:, 0:RHS] + both[:, RHS:]
+            pq[...] += both[0:PRIM]
+            ems[pl.ds(f, 1)] = both[PRIM:][None]
+            exists, _ = where_is(f)
+
+            @pl.when(exists)
+            def _():
+                em_copy(f, other(f)).start()
+
+            return carry
+
+        lax.fori_loop(0, 4, one, 0)
+
+    def early_launch():
+        for f in range(4):
+            exists, _ = where_is(f)
+
+            @pl.when(exists)
+            def _():
+                arrival = em_copy(f, f)
+                arrival.wait_recv()
+                arrival.wait_send()
+
+        coarse(1, pq[...] + ((emr[0] + emr[1]) + (emr[2] + emr[3])))
 
     def step(it, carry):
         acc[...] = jnp.zeros_like(acc)
         first = 1 + 2 * it
         second = 2 + 2 * it
 
-        coarse(it)
+        pl.when(it == 0)(lambda: coarse(0, dot(basis[...], wb[...])))
 
         def local(i, carry):
             f = 3 - i
             t[rows(f)] = dot(lv[rows(f)], wb[...]) * weight(f)
-            send_face(first, f, t)
-            return carry
-
-        lax.fori_loop(0, 4, local, 0)
-        solve_coarse(it)
-        own_high, own_low = halves(pk[...])
+            order_face(f, t)
+
+            @pl.when(jnp.logical_and(i < 2, it == 0))
+            def _():
+                start_face(first, f, 0, CUT_LOCAL)
+
+            @pl.when(jnp.logical_and(i < 2, it > 0))
+            def _():
+                start_face(first, f, 0, CUT_AGAIN)
+
+            @pl.when(i >= 2)
+            def _():
+                start_face(first, f, 0, FACE)
+
+            return carry
+
+        lax.fori_loop(0, 2, local, 0)
+        pl.when(it > 0)(lambda: solve_row(1, CUT_AGAIN))
+        lax.fori_loop(2, 4, local, 0)
+
+        @pl.when(it == 0)
+        def _():
+            build_late()
+            solve_row(0, CUT_LOCAL)
+            build_rank()
+
+        solve_coarsest(it)
+        pl.when(it > 0)(lambda: pick(it))
 
         def settle(f, carry):
             await_face(first, f)
-            near_high, near_low = halves(
-                pkr[pl.ds(it, 1), pl.ds(f, 1)].reshape(PRIM, RHS)
-            )
-            stack = jnp.concatenate([own_high, own_low, near_high, near_low], axis=0)
+            value = t[rows(f)] + face_of(first, f)
+            zz[pl.ds(it, 1), rows(f)] = value[None]
+            wb[rows(f)] = value.astype(BF16)
+            return carry
+
+        lax.fori_loop(0, 4, settle, 0)
+
+        def stiff(i, carry):
+            f = 3 - i
+            t[rows(f)] = dot(sv[rows(f)], wb[...])
+            return carry
+
+        lax.fori_loop(0, 2, stiff, 0)
+        pl.when(it == 0)(lambda: pick(it))
+        lax.fori_loop(2, 4, stiff, 0)
+        await_picks(it)
+        picks = [pk[...]] + [pkr[it, k] for k in range(4)]
+        picks = jnp.concatenate(picks + [jnp.zeros((3 * PRIM, RHS), F32)], axis=0)
+        high, low = halves(picks)
+        pkhl[0:256] = high
+        pkhl[256:512] = high
+        pkhl[512:768] = low
+
+        def complete(i, carry):
+            f = 3 - i
+            near = pl.ds(pl.multiple_of(PRIM * (f + 1), PRIM), PRIM)
+            near_low = pl.ds(pl.multiple_of(PRIM * (f + 1) + 512, PRIM), PRIM)
+            stack = jnp.concatenate(
+                [pkhl[0:PRIM], pkhl[512 : 512 + PRIM], pkhl[near], pkhl[near_low]], axis=0
+            )
             rank = dot(cmat[pl.ds(f, 1)].reshape(FACE, 128), stack)
-            value = t[rows(f)] + face_of(first, f) + rank
+            value = zz[pl.ds(it, 1), rows(f)].reshape(FACE, RHS) + rank
             zz[pl.ds(it, 1), rows(f)] = value[None]
+            image = (
+                t[rows(f)]
+                + dot(sc[rows(f)], pkhl[0:512])
+                + dot(sc[rows(f), 0:256], pkhl[512:768])
+            )
+            t[rows(f)] = image
+
+            order_face(f, t)
+
+            @pl.when(i < 2)
+            def _():
+                start_face(second, f, 0, CUT_STIFF)
+
+            @pl.when(i >= 2)
+            def _():
+                start_face(second, f, 0, CUT_SIDE)
+
             wide = weight(f)
             acc[0] += wide * eighths(value * r[rows(f)])
             acc[1] += wide * eighths(value * q[rows(f)])
-            return carry
-
-        lax.fori_loop(0, 4, settle, 0)
-
-        def narrow(f, carry):
-            wb[rows(f)] = zz[pl.ds(it, 1), rows(f)].reshape(FACE, RHS).astype(BF16)
-            return carry
-
-        lax.fori_loop(0, 4, narrow, 0)
-
-        def stiff(i, carry):
-            f = 3 - i
-            value = dot(sv[rows(f)], wb[...])
-            t[rows(f)] = value
-            send_face(second, f, t)
-            acc[2] += eighths(value * zz[pl.ds(it, 1), rows(f)].reshape(FACE, RHS))
-            acc[3] += eighths(value * zz[0, rows(f)])
-            return carry
-
-        lax.fori_loop(0, 4, stiff, 0)
-        red[...] = jnp.zeros_like(red)
+            acc[2] += eighths(image * value)
+            acc[3] += eighths(image * zz[0, rows(f)])
+            return carry
+
+        lax.fori_loop(0, 4, complete, 0)
         for k in range(4):
-            red[k : k + 1] = column_sums(acc[k])
+            total = column_sums(acc[k])
+            redz[k : k + 1] = total[:, 0:128]
+            redz[4 + k : 5 + k] = total[:, 128:256]
+        redzr[pl.ds(it, 1), pl.ds(g, 1)] = redz[...][None, None]
+
+        def redz_copy(k):
+            return pltpu.make_async_remote_copy(
+                src_ref=redz,
+                dst_ref=redzr.at[it, g],
+                send_sem=redz_sem.at[it, 0],
+                recv_sem=redz_sem.at[it, 1],
+                device_id=((g + k) % ROWS, c),
+                device_id_type=MESH,
+            )
+
+        for k in range(1, ROWS):
+            redz_copy(k).start()
+        pl.when(it == 0)(early_send)
+        start_face(second, 3, CUT_STIFF, FACE)
+        start_face(second, 2, CUT_STIFF, FACE)
+        wait_bytes(
+            redzr.at[it, pl.ds(0, ROWS - 1)], redz_sem.at[it, 0], redz_sem.at[it, 1], z_peer
+        )
+        red[...] = jnp.sum(redzr[pl.ds(it, 1)].reshape(ROWS, 8, 128), axis=0)
 
         def red_copy(k):
             return pltpu.make_async_remote_copy(
@@ -512,30 +715,15 @@
             return carry
 
         lax.fori_loop(1, COLS, start, 0)
+        pl.when(it == 0)(early_launch)
+        start_face(second, 1, CUT_SIDE, FACE)
+        start_face(second, 0, CUT_SIDE, FACE)
         redr[pl.ds(it, 1), pl.ds(c, 1)] = red[...][None, None]
         wait_bytes(
             redr.at[it, pl.ds(0, COLS - 1)], red_sem.at[it, 0], red_sem.at[it, 1], row_peer
         )
-        row_sum = jnp.sum(redr[pl.ds(it, 1)].reshape(COLS, 8, RHS), axis=0)
-        redz[...] = row_sum
-        redzr[pl.ds(it, 1), pl.ds(g, 1)] = row_sum[None, None]
-
-        def redz_copy(k):
-            return pltpu.make_async_remote_copy(
-                src_ref=redz,
-                dst_ref=redzr.at[it, g],
-                send_sem=redz_sem.at[it, 0],
-                recv_sem=redz_sem.at[it, 1],
-                device_id=((g + k) % ROWS, c),
-                device_id_type=MESH,
-            )
-
-        for k in range(1, ROWS):
-            redz_copy(k).start()
-        wait_bytes(
-            redzr.at[it, pl.ds(0, ROWS - 1)], redz_sem.at[it, 0], redz_sem.at[it, 1], z_peer
-        )
-        sums = jnp.sum(redzr[pl.ds(it, 1)].reshape(ROWS, 8, RHS), axis=0)
+        sums = jnp.sum(redr[pl.ds(it, 1)].reshape(COLS, 8, 128), axis=0)
+        sums = jnp.concatenate([sums[0:4], sums[4:8]], axis=1)
         rz = sums[0:1]
         beta = jnp.where(it > 0, rz / scal[0:1], 0.0)
         curv = sums[2:3] + beta * (sums[1:2] + sums[3:4]) + beta * beta * scal[1:2]
@@ -602,15 +790,21 @@
             pltpu.VMEM((4, FACE, 128), BF16),
             pltpu.VMEM((4, PRIM, FACE), F32),
             pltpu.VMEM((4, PRIM, FACE), F32),
-            pltpu.VMEM((BLOCK + 16, NQ), F32),
-            pltpu.VMEM((COLS, BLOCK + 16, NQ), F32),
+            pltpu.VMEM((8, 128), F32),
+            pltpu.VMEM((COLS, 8, 128), F32),
+            pltpu.VMEM((COLS, BLOCK, NQ), F32),
             pltpu.VMEM((4, BLOCK, NCG), F32),
             pltpu.VMEM((NCG, NCG), BF16),
             pltpu.VMEM((NCG, 128), BF16),
             pltpu.VMEM((256, NCG), BF16),
             pltpu.VMEM((256, NCG), BF16),
-            pltpu.VMEM((128, NQ), F32),
+            pltpu.VMEM((PRIM, NQ), F32),
             pltpu.VMEM((NCG, 128), F32),
+            pltpu.VMEM((IFACE, 256), BF16),
+            pltpu.VMEM((IFACE, 512), BF16),
+            pltpu.VMEM((64, 128), F32),
+            pltpu.VMEM((ITERS, 4, 64, 128), F32),
+            pltpu.VMEM((768, RHS), BF16),
             pltpu.VMEM((4, 16, 128), F32),
             pltpu.VMEM((ITERS, COLS, 16, 128), F32),
             pltpu.VMEM((64, 128), F32),
@@ -619,16 +813,22 @@
             pltpu.VMEM((ITERS, COLS, 16, 128), F32),
             pltpu.VMEM((PRIM, RHS), F32),
             pltpu.VMEM((ITERS, 4, PRIM, RHS), F32),
-            pltpu.VMEM((8, RHS), F32),
-            pltpu.VMEM((ITERS, COLS, 8, RHS), F32),
-            pltpu.VMEM((8, RHS), F32),
-            pltpu.VMEM((ITERS, ROWS, 8, RHS), F32),
+            pltpu.VMEM((8, 128), F32),
+            pltpu.VMEM((ITERS, COLS, 8, 128), F32),
+            pltpu.VMEM((8, 128), F32),
+            pltpu.VMEM((ITERS, ROWS, 8, 128), F32),
             pltpu.VMEM((4, 8, RHS), F32),
             pltpu.VMEM((8, RHS), F32),
+            pltpu.VMEM((4, 2 * PRIM, FACE), BF16),
+            pltpu.VMEM((4, PRIM, RHS), F32),
+            pltpu.VMEM((4, PRIM, RHS), F32),
+            pltpu.VMEM((PRIM, RHS), F32),
+            pltpu.VMEM((PRIM, RHS), F32),
             dma((4,)), dma((2,)), dma((4,)), dma((1 + 2 * ITERS, 4)),
-            dma((4,)), dma((4,)), dma((2,)), dma((2,)),
-            dma((ITERS, 2)), dma((ITERS, 2)), dma((ITERS, 2)),
+            dma((4,)), dma((4,)), dma((2,)), dma((2,)), dma((2,)),
+            dma((ITERS, 2)), dma((ITERS, 2)), dma((ITERS, 2)), dma((ITERS, 2)),
             dma((4,)), dma((ITERS, 4)), dma((ITERS, 2)), dma((ITERS, 2)), dma((2,)),
+            dma((4,)), dma((4,)),
         ],
         compiler_params=pltpu.CompilerParams(
             collective_id=0, has_side_effects=True, vmem_limit_bytes=63 * 1024 * 1024

time: 141 us -> 115 us (0.82)
  Pallas kernels: 136 us -> 110 us
    pallas_call x1, Pallas kernels: 136 us -> 110 us  [body(): pl.pallas_call(kernel, out_shape=(out, out), in_specs=[anywhere] * 3 + [n...]
where the time goes in v2:
time: 115 us
  Pallas kernels  110 us (96%)
  local copies, waits for them, and re-layouts  4.52 us (4%)
    pallas_call x1, Pallas kernels, body(): pl.pallas_call(kernel, out_shape=(out, out), in_specs=[anywhere] * 3 + [n...  110 us
    unnamed x4, local copies, waits for them, and re-layouts  4.52 us

profile of v2, /device:TPU:1, one launch (start us, length us, event | category | flops | bytes accessed | tf_op | source)
XLA Modules:
  0.0 114.8 jit_solution(10158565659805009811)
XLA Ops:
  0.6 109.6 %shard_map.104 = (f32[2048,256]{1,0:T(8,128)}, f32[2048,256]{1,0:T(8,128)}) custom-call(f32[2048,256]{1,0:T(8,128)} %bitcast.11, bf16[2048,2048]{1,0:T(8,128)(2,1)} %bitcast.9, bf16[2048,2048]{1,0:T(8,128)(2,1)} %bitcast.10, s32[4,512]{1,0:T(4,128)} %bitcast.17, bf16[32,2048]{1,0:T(8,128)(2,1)} %bitcast.14, s32[1,32]{1,0:T(1,128)} %index.1, ...), custom_call_target="tpu_custom_call" | custom-call | tf_op jit(solution)/shard_map/pallas_call | solution.py:774
  110.3 0.0 copy-start
  110.3 3.2 %copy.13 = f32[1,2048,256]{2,1,0:T(8,128)} copy(f32[1,2048,256]{2,1,0:T(8,128)} %bitcast.13) | data formatting | bytes 4194304
  113.5 0.0 copy-done
  113.5 1.3 %copy.14 = f32[1,2048,256]{2,1,0:T(8,128)} copy(f32[1,2048,256]{2,1,0:T(8,128)S(1)} %bitcast.12) | data formatting | bytes 4194304
Async XLA Ops:
  110.3 3.2 %copy-start = (f32[2048,256]{1,0:T(8,128)S(1)}, f32[2048,256]{1,0:T(8,128)}, u32[]{:S(2)}) copy-start(f32[2048,256]{1,0:T(8,128)} %get-tuple-element.5) | copy-start | bytes 6291460

commit v3 on v2

--- a/solution.py
+++ b/solution.py
@@ -22,7 +22,7 @@
 BLOCK = NCG // COLS
 CUT_LOCAL = 384
 CUT_AGAIN = 128
-CUT_STIFF = 128
+CUT_STIFF = 160
 CUT_SIDE = 256
 
 
@@ -575,6 +575,11 @@
 
         coarse(1, pq[...] + ((emr[0] + emr[1]) + (emr[2] + emr[3])))
 
+    x_copy = pltpu.make_async_copy(zz.at[0], x_out, out_sem.at[4])
+
+    def r_copy(f):
+        return pltpu.make_async_copy(r.at[rows(f)], r_out.at[rows(f)], out_sem.at[f])
+
     def step(it, carry):
         acc[...] = jnp.zeros_like(acc)
         first = 1 + 2 * it
@@ -734,6 +739,18 @@
         scal[2:3] = alpha
         scal[4:5] = beta
 
+        @pl.when(it == ITERS - 1)
+        def _():
+            held = scal[3:4] + alpha * beta
+
+            def finish(f, carry):
+                zz[0, rows(f)] = held * zz[0, rows(f)] + alpha * zz[1, rows(f)]
+                return carry
+
+            lax.fori_loop(0, 4, finish, 0)
+            x_copy.start()
+
+
         def update(f, carry):
             await_face(second, f)
             image = t[rows(f)] + face_of(second, f) + beta * q[rows(f)]
@@ -741,25 +758,19 @@
             value = r[rows(f)] - alpha * image
             r[rows(f)] = value
             wb[rows(f)] = (value * weight(f)).astype(BF16)
+
+            @pl.when(it == ITERS - 1)
+            def _():
+                r_copy(f).start()
+
             return carry
 
         lax.fori_loop(0, 4, update, 0)
         return carry
 
     lax.fori_loop(0, ITERS, step, 0)
-    alpha = scal[2:3]
-    held = scal[3:4] + alpha * scal[4:5]
-
-    def finish(f, carry):
-        t[rows(f)] = held * zz[0, rows(f)] + alpha * zz[1, rows(f)]
-        return carry
-
-    r_copy = pltpu.make_async_copy(r, r_out, out_sem.at[0])
-    r_copy.start()
-    lax.fori_loop(0, 4, finish, 0)
-    x_copy = pltpu.make_async_copy(t, x_out, out_sem.at[1])
-    x_copy.start()
-    r_copy.wait()
+    for f in range(4):
+        r_copy(f).wait()
     x_copy.wait()
 
 
@@ -827,7 +838,7 @@
             dma((4,)), dma((2,)), dma((4,)), dma((1 + 2 * ITERS, 4)),
             dma((4,)), dma((4,)), dma((2,)), dma((2,)), dma((2,)),
             dma((ITERS, 2)), dma((ITERS, 2)), dma((ITERS, 2)), dma((ITERS, 2)),
-            dma((4,)), dma((ITERS, 4)), dma((ITERS, 2)), dma((ITERS, 2)), dma((2,)),
+            dma((4,)), dma((ITERS, 4)), dma((ITERS, 2)), dma((ITERS, 2)), dma((5,)),
             dma((4,)), dma((4,)),
         ],
         compiler_params=pltpu.CompilerParams(

time: 115 us -> 114 us (level)
  no operation moved by 1% of the time
where the time goes in v3:
time: 114 us
  Pallas kernels  109 us (96%)
  local copies, waits for them, and re-layouts  4.52 us (4%)
    pallas_call x1, Pallas kernels, body(): pl.pallas_call(kernel, out_shape=(out, out), in_specs=[anywhere] * 3 + [n...  109 us
    unnamed x4, local copies, waits for them, and re-layouts  4.52 us

profile of v3, /device:TPU:1, one launch (start us, length us, event | category | flops | bytes accessed | tf_op | source)
XLA Modules:
  0.0 114.0 jit_solution(10701424257639603502)
XLA Ops:
  0.6 108.9 %shard_map.104 = (f32[2048,256]{1,0:T(8,128)}, f32[2048,256]{1,0:T(8,128)}) custom-call(f32[2048,256]{1,0:T(8,128)} %bitcast.11, bf16[2048,2048]{1,0:T(8,128)(2,1)} %bitcast.9, bf16[2048,2048]{1,0:T(8,128)(2,1)} %bitcast.10, s32[4,512]{1,0:T(4,128)} %bitcast.17, bf16[32,2048]{1,0:T(8,128)(2,1)} %bitcast.14, s32[1,32]{1,0:T(1,128)} %index.1, ...), custom_call_target="tpu_custom_call" | custom-call | tf_op jit(solution)/shard_map/pallas_call | solution.py:785
  109.5 0.0 copy-start
  109.5 3.2 %copy.13 = f32[1,2048,256]{2,1,0:T(8,128)} copy(f32[1,2048,256]{2,1,0:T(8,128)} %bitcast.13) | data formatting | bytes 4194304
  112.7 0.0 copy-done
  112.7 1.3 %copy.14 = f32[1,2048,256]{2,1,0:T(8,128)} copy(f32[1,2048,256]{2,1,0:T(8,128)S(1)} %bitcast.12) | data formatting | bytes 4194304
Async XLA Ops:
  109.5 3.2 %copy-start = (f32[2048,256]{1,0:T(8,128)S(1)}, f32[2048,256]{1,0:T(8,128)}, u32[]{:S(2)}) copy-start(f32[2048,256]{1,0:T(8,128)} %get-tuple-element.5) | copy-start | bytes 6291460
